TPU v7x, 16 devices: a whole 2x2x2 slice. The times are simulated.
16 devices in a mesh: dp: 16 (over z, y, x, core).
Axes of the slice: x: 2, y: 2, z: 2, core: 2. Of those that a mesh axis runs over, the one named last changes fastest.
Arguments:
- local_grads: bfloat16 [16, 32768, 768], P('dp')
- master: float32 [32768, 768], P('dp')
- mom_first: float32 [32768, 768], P('dp')
- mom_second: float32 [32768, 768], P('dp')
- learn_rate: float32 [], replicated
Outputs:
- output 1: float32 [32768, 768], P('dp')
- output 2: float32 [32768, 768], P('dp')
- output 3: float32 [32768, 768], P('dp')
- output 4: bfloat16 [32768, 768], replicated
All inputs are finite; a program needn't handle non-finite values.
Results may differ from a plain program's by a relative error of at most 0.001.
Values are sent between devices in bfloat16 or wider.
A program may use at most 1 GiB of HBM per device.

v0:
```python
import jax
import jax.numpy as jnp
from jax import lax
from jax.sharding import PartitionSpec as P, NamedSharding

LAYERS = 2
MIX_RANK = 32
DECAY_RANK = 64
ADAM_STEP = 10


def layout_runs(model_width, total_rows):
    ffn_width = 7 * model_width // 2
    layer_rows = 6 * model_width + 2 * ffn_width + 16 + 10 * MIX_RANK + 2 * DECAY_RANK
    vocab_rows = (total_rows - LAYERS * layer_rows - 4) // 2
    base_rule = (1.0, 0.0)
    decay_rule = (1.0, 0.1)
    time_rule = (2.0, 0.0)
    pieces = [(vocab_rows, decay_rule)]
    for layer_idx in range(LAYERS):
        lead_rows = 12 if layer_idx == 0 else 10
        pieces = pieces + [(lead_rows + 10 * MIX_RANK, base_rule), (1, time_rule), (2 * DECAY_RANK, base_rule), (1, time_rule), (5 * model_width, decay_rule), (4, base_rule), (2 * ffn_width + model_width, decay_rule)]
    pieces = pieces + [(2, base_rule), (vocab_rows, decay_rule)]
    run_starts = []
    next_row = 0
    for run_len, run_rule in pieces:
        run_starts.append(next_row)
        next_row = next_row + run_len
    lr_values = [run_rule[0] for run_len, run_rule in pieces]
    decay_values = [run_rule[1] for run_len, run_rule in pieces]
    return run_starts, lr_values, decay_values


def row_rules(row_ids, model_width, total_rows):
    run_starts, lr_values, decay_values = layout_runs(model_width, total_rows)
    later_starts = jnp.asarray(run_starts[1:], jnp.int32)
    run_index = jnp.sum((row_ids[:, None] >= later_starts[None, :]).astype(jnp.int32), axis=1)
    lr_factor = jnp.asarray(lr_values, jnp.float32)[run_index]
    decay_rate = jnp.asarray(decay_values, jnp.float32)[run_index]
    return lr_factor[:, None], decay_rate[:, None]


def adam_rows(grad_rows, master_rows, first_rows, second_rows, clip_scale, learn_rate, lr_factor, decay_rate):
    clipped = grad_rows * clip_scale
    new_first = 0.9 * first_rows + 0.1 * clipped
    new_second = 0.99 * second_rows + 0.01 * (clipped * clipped)
    first_hat = new_first / (1.0 - 0.9 ** ADAM_STEP)
    second_hat = new_second / (1.0 - 0.99 ** ADAM_STEP)
    step_size = learn_rate * lr_factor
    new_master = master_rows - step_size * (first_hat / (jnp.sqrt(second_hat) + 1e-8) + decay_rate * master_rows)
    return new_master, new_first, new_second


def solution(mesh):
    dev_count = mesh.shape['dp']

    def device_step(local_grads, master, mom_first, mom_second, learn_rate):
        shard_rows = master.shape[0]
        model_width = master.shape[1]
        total_rows = shard_rows * dev_count
        grad_shard = lax.psum_scatter(local_grads[0].astype(jnp.float32), 'dp', scatter_dimension=0, tiled=True) / dev_count
        square_sum = lax.psum(jnp.sum(grad_shard * grad_shard), 'dp')
        clip_scale = jnp.minimum(1.0, 1.0 / (jnp.sqrt(square_sum) + 1e-6))
        row_ids = lax.axis_index('dp') * shard_rows + lax.iota(jnp.int32, shard_rows)
        lr_factor, decay_rate = row_rules(row_ids, model_width, total_rows)
        new_master, new_first, new_second = adam_rows(grad_shard, master, mom_first, mom_second, clip_scale, learn_rate, lr_factor, decay_rate)
        working = lax.all_gather(new_master.astype(jnp.bfloat16), 'dp', axis=0, tiled=True)
        return new_master, new_first, new_second, working

    return jax.shard_map(device_step, mesh=mesh, in_specs=(P('dp', None, None), P('dp', None), P('dp', None), P('dp', None), P()), out_specs=(P('dp', None), P('dp', None), P('dp', None), P(None, None)), check_vma=False)
```

profile of v0, /device:TPU:0, one launch (start us, length us, event | category | flops | bytes accessed | tf_op | source)
XLA Modules:
  0.0 804.9 jit_solution(9523943721790824276)
XLA Ops:
  7.2 0.0 reduce-scatter.4.cloned.1.call-start
  7.2 49.8 %bitcast_convert_fusion = f32[32768,768]{1,0:T(8,128)} fusion(bf16[1,32768,768]{2,1,0:T(8,128)(2,1)} %param.8), kind=kLoop, calls=%fused_computation | loop fusion | flops 25165824 | bytes 150994944 | tf_op jit(solution)/shard_map/convert_element_type | solution.py:61
  57.0 0.0 copy-start
  57.0 0.0 reduce-scatter.4.cloned.1.call-update
  57.1 0.0 all-gather.2.cloned.1.call-start
  57.8 0.0 copy-done
  57.8 0.1 convert_reduce_fusion
  57.9 0.2 compare_reduce_fusion.9
  58.2 465.8 %reduce-scatter.4.cloned.1.call-done = f32[2048,768]{1,0:T(8,128)} async-done(((f32[32768,768]{1,0:T(8,128)}), f32[2048,768]{1,0:T(8,128)}) %reduce-scatter.4.cloned.1.call-update) | async-done | bytes 6291472
  524.0 5.0 multiply_reduce_fusion
  529.0 32.0 %psum.7 = f32[]{:T(128)} all-reduce(f32[]{:T(128)} %multiply_reduce_fusion), channel_id=1, replica_groups=mesh['dp'=16] {'dp'}, use_global_device_ids=true, to_apply=%region_3.0 | all-reduce | flops 1 | bytes 8 | tf_op jit(solution)/shard_map/psum | solution.py:62
  561.7 14.9 %fusion = (bf16[2048,768]{1,0:T(8,128)(2,1)}, f32[2048,768]{1,0:T(8,128)}, f32[2048,768]{1,0:T(8,128)}, f32[2048,768]{1,0:T(8,128)}) fusion(f32[2048,768]{1,0:T(8,128)} %param.9, f32[2048]{0:T(1024)S(1)} %get-tuple-element.21, f32[2048]{0:T(1024)S(1)} %get-tuple-element.20, f32[2048,768]{1,0:T(8,128)} %reduce-scatter.4.cloned.1.call-done, f32[]{:T(128)S(6)} %mul.75, ...), kind=kLoop, calls=%fused_computation.31 | loop fusion | flops 26738688 | bytes 47202308 | tf_op jit(solution)/shard_map/convert_element_type | solution.py:67
  576.6 0.0 all-gather.2.cloned.1.call-update
  576.6 187.1 %all-gather.2.cloned.1.call-done = bf16[32768,768]{1,0:T(8,128)(2,1)} async-done(((bf16[2048,768]{1,0:T(8,128)(2,1)}), bf16[32768,768]{1,0:T(8,128)(2,1)}) %all-gather.2.cloned.1.call-update) | async-done | bytes 50331664 | tf_op jit(solution)/shard_map/all_gather | solution.py:67
  763.7 34.3 %copy.14 = bf16[32768,768]{1,0:T(8,128)(2,1)} copy(bf16[32768,768]{1,0:T(8,128)(2,1)} %all-gather.2.cloned.1.call-done) | data formatting | bytes 100663296
  (4 shorter events, 0.1 us)
Async XLA Ops:
  7.2 516.8 %reduce-scatter.4.cloned.1.call-start = ((), (), s32[]{:S(2)}) async-start(), calls=%async_computation.2 | async-start | bytes 106954752
  57.0 0.7 copy-start
  57.1 706.7 %all-gather.2.cloned.1.call-start = ((), (), s32[]{:S(2)}) async-start(), calls=%async_computation.1 | async-start | bytes 53477376 | tf_op jit(solution)/shard_map/all_gather | solution.py:67
Sparse Core Ops, SparseCore 0:
  57.2 466.7 reduce-scatter.3
  576.7 186.9 all-gather.1
where the time goes:
time: 805 us
  waiting for transfers between devices  653 us (81%)
  other arithmetic  70.1 us (9%)
  local copies, waits for them, and re-layouts  34.3 us (4%)
  blocking collectives  32 us (4%)
  between operations  15.5 us (2%)
    unnamed x3, waiting for transfers between devices  466 us
    all_gather x1, waiting for transfers between devices, device_step(): lax.all_gather(new_master.astype(jnp.bfloat16), 'dp', axis=0, tiled=True)  187 us
    convert_element_type x1, other arithmetic, device_step(): local_grads[0].astype(jnp.float32)  49.8 us
    unnamed x3, local copies, waits for them, and re-layouts  34.3 us
    psum x1, blocking collectives, device_step(): square_sum = lax.psum(jnp.sum(grad_shard * grad_shard), 'dp')  32 us
  transfers between devices with their start and end apart: 2, of which 2 were waited for; matrix products, arithmetic and copies ran while one was open for 0% of the time, Pallas kernels for 0%

commit v1 on v0

--- a/solution.py
+++ b/solution.py
@@ -1,12 +1,21 @@
+import functools
+
 import jax
 import jax.numpy as jnp
 from jax import lax
-from jax.sharding import PartitionSpec as P, NamedSharding
+from jax.experimental import pallas as pl
+from jax.experimental.pallas import tpu as pltpu
+from jax.sharding import PartitionSpec as P
 
 LAYERS = 2
 MIX_RANK = 32
 DECAY_RANK = 64
 ADAM_STEP = 10
+
+AXES = 3
+CHUNKS = 4
+SLOTS = 3
+MESH = pl.DeviceIdType.MESH
 
 
 def layout_runs(model_width, total_rows):
@@ -51,6 +60,226 @@
     return new_master, new_first, new_second
 
 
+def bit_flip(index, mask):
+    flipped = index
+    for bit in range(4):
+        step = 1 << bit
+        if mask & step:
+            flipped = flipped + step - 2 * step * ((index // step) % 2)
+    return flipped
+
+
+def dest_mask(e, k):
+    mask = 0
+    for place in range(AXES):
+        if e >> (2 - place) & 1:
+            mask |= 1 << ((k + place) % AXES)
+    return mask
+
+
+def reduce_kernel(grads, g_out, c_out, pairs, landed, stage, own_buf, pair_buf, part_buf, norm_buf,
+                  pair_ssem, pair_rsem, send_sem, recv_sem, own_sem, pairl_sem, norm_ssem, norm_rsem, g_sem):
+    me = lax.axis_index('dp')
+    chip, core = me // 2, me % 2
+    partner = bit_flip(me, 1)
+    rows = g_out.shape[0]
+    third = g_out.shape[1] // AXES
+    part_rows = rows // CHUNKS
+    devices = norm_buf.shape[0]
+
+    def unit_row(j, k, parity):
+        row = 0
+        flip = chip
+        e = 7 - j
+        for place in range(AXES):
+            step = 1 << ((k + place) % AXES)
+            want = (e // (1 << (2 - place))) % 2
+            bit = (chip // step) % 2
+            flip = flip + want * (step - 2 * step * bit)
+        return (2 * flip + parity) * rows + row
+
+    def pair_copy(j, k):
+        return pltpu.make_async_remote_copy(
+            src_ref=grads.at[0, pl.ds(pl.multiple_of(unit_row(j, k, 1 - core), rows), rows), pl.ds(k * third, third)],
+            dst_ref=pairs.at[j, k],
+            send_sem=pair_ssem.at[j, k],
+            recv_sem=pair_rsem.at[j, k],
+            device_id=(partner,),
+            device_id_type=MESH)
+
+    def own_load(s, k):
+        j, i = s // CHUNKS, s % CHUNKS
+        row = pl.multiple_of(unit_row(j, k, core) + i * part_rows, part_rows)
+        return pltpu.make_async_copy(
+            grads.at[0, pl.ds(row, part_rows), pl.ds(k * third, third)], own_buf.at[s % 2, k], own_sem.at[s % 2, k])
+
+    def pair_load(s, k):
+        j, i = s // CHUNKS, s % CHUNKS
+        return pltpu.make_async_copy(
+            pairs.at[j, k, pl.ds(pl.multiple_of(i * part_rows, part_rows), part_rows)], pair_buf.at[s % 2, k], pairl_sem.at[s % 2, k])
+
+    def piece_copy(j, i, k, slot, axis):
+        return pltpu.make_async_remote_copy(
+            src_ref=stage.at[k, slot],
+            dst_ref=landed.at[j, k, pl.ds(pl.multiple_of(i * part_rows, part_rows), part_rows)],
+            send_sem=send_sem.at[k, slot],
+            recv_sem=recv_sem.at[j, k, i],
+            device_id=(bit_flip(me, 2 << axis),),
+            device_id_type=MESH)
+
+    def start_loads(s):
+        for k in range(AXES):
+            @pl.when(s % CHUNKS == 0)
+            def _():
+                pair_copy(s // CHUNKS, k).wait_recv()
+            own_load(s, k).start()
+            pair_load(s, k).start()
+
+    for j in range(8):
+        for k in range(AXES):
+            pair_copy(j, k).start()
+
+    total_steps = 8 * CHUNKS
+    start_loads(0)
+
+    def step(s, phase):
+        j, i = s // CHUNKS, s % CHUNKS
+
+        @pl.when(s + 1 < total_steps)
+        def _():
+            start_loads(s + 1)
+
+        if phase == 1:
+            sources = []
+        elif phase == 2:
+            sources = [j - 4]
+        elif phase == 3:
+            sources = [2, 4]
+        else:
+            sources = [3, 5, 6]
+        slot = s % SLOTS
+        base = pl.multiple_of(i * part_rows, part_rows)
+        for k in range(AXES):
+            own_load(s, k).wait()
+            pair_load(s, k).wait()
+            for source in sources:
+                piece_copy(source, i, k, 0, 0).wait_recv()
+            if phase < 4:
+                @pl.when(s >= SLOTS)
+                def _():
+                    piece_copy(0, 0, k, slot, 0).wait_send()
+            group = 64
+
+            def add_rows(r, carry):
+                lo = pl.multiple_of(r * group, group)
+                value = own_buf[s % 2, k, pl.ds(lo, group)].astype(jnp.float32) + pair_buf[s % 2, k, pl.ds(lo, group)].astype(jnp.float32)
+                for source in sources:
+                    value = value + landed[source, k, pl.ds(base + lo, group)]
+                if phase < 4:
+                    stage[k, slot, pl.ds(lo, group)] = value
+                    return carry
+                value = value * (1.0 / devices)
+                landed[0, k, pl.ds(base + lo, group)] = value
+                return carry + jnp.sum((value * value).reshape(group // 8, 8, third), axis=0)
+
+            if phase < 4:
+                lax.fori_loop(0, part_rows // group, add_rows, 0)
+            else:
+                part_buf[...] += lax.fori_loop(0, part_rows // group, add_rows, jnp.zeros((8, third), jnp.float32))
+        for k in range(AXES):
+            if phase < 4:
+                piece_copy(j, i, k, slot, (k + phase - 1) % AXES).start()
+            else:
+                pltpu.make_async_copy(
+                    landed.at[0, k, pl.ds(base, part_rows)],
+                    g_out.at[pl.ds(base, part_rows), pl.ds(k * third, third)], g_sem.at[k, i]).start()
+
+    part_buf[...] = jnp.zeros_like(part_buf)
+    for phase, lo, hi in ((1, 0, 4), (2, 4, 6), (3, 6, 7), (4, 7, 8)):
+        def run(s, carry, phase=phase):
+            step(s, phase)
+            return carry
+        lax.fori_loop(lo * CHUNKS, hi * CHUNKS, run, 0)
+
+    part_buf[:, :128] = part_buf[:, :128] + part_buf[:, 128:]
+    norm_buf[me] = part_buf[:, :128]
+
+    def norm_copy(d):
+        return pltpu.make_async_remote_copy(
+            src_ref=part_buf.at[:, pl.ds(0, 128)],
+            dst_ref=norm_buf.at[me],
+            send_sem=norm_ssem.at[d],
+            recv_sem=norm_rsem.at[me],
+            device_id=((me + d) % devices,),
+            device_id_type=MESH)
+
+    def norm_recv(d):
+        sender = (me + devices - d) % devices
+        return pltpu.make_async_remote_copy(
+            src_ref=part_buf.at[:, pl.ds(0, 128)],
+            dst_ref=norm_buf.at[sender],
+            send_sem=norm_ssem.at[d],
+            recv_sem=norm_rsem.at[sender],
+            device_id=(partner,),
+            device_id_type=MESH)
+
+    for d in range(1, devices):
+        norm_copy(d).start()
+    for last in range(SLOTS):
+        for k in range(AXES):
+            piece_copy(0, 0, k, last, 0).wait_send()
+    for j in range(8):
+        for k in range(AXES):
+            pair_copy(j, k).wait_send()
+    for i in range(CHUNKS):
+        for k in range(AXES):
+            pltpu.make_async_copy(
+                landed.at[0, k, pl.ds(i * part_rows, part_rows)],
+                g_out.at[pl.ds(i * part_rows, part_rows), pl.ds(k * third, third)], g_sem.at[k, i]).wait()
+    for d in range(1, devices):
+        norm_copy(d).wait_send()
+    for d in range(1, devices):
+        norm_recv(d).wait_recv()
+    square_sum = jnp.sum(jnp.sum(norm_buf[...], axis=0), keepdims=True)
+    c_out[...] = jnp.broadcast_to(jnp.minimum(1.0, 1.0 / (jnp.sqrt(square_sum) + 1e-6)), c_out.shape)
+
+
+def reduce_scatter(local_grads, devices):
+    total_rows, width = local_grads.shape[1:]
+    rows, third = total_rows // devices, width // AXES
+    any_spec = pl.BlockSpec(memory_space=pl.ANY)
+    f32, bf16 = jnp.float32, jnp.bfloat16
+    part_rows = rows // CHUNKS
+    g, scale, _ = pl.pallas_call(
+        reduce_kernel,
+        out_shape=(jax.ShapeDtypeStruct((rows, width), f32),
+                   jax.ShapeDtypeStruct((8, 128), f32),
+                   jax.ShapeDtypeStruct((8, AXES, rows, third), bf16)),
+        in_specs=[any_spec],
+        out_specs=(any_spec, pl.BlockSpec(memory_space=pltpu.VMEM), any_spec),
+        scratch_shapes=[
+            pltpu.VMEM((7, AXES, rows, third), f32),
+            pltpu.VMEM((AXES, SLOTS, part_rows, third), f32),
+            pltpu.VMEM((2, AXES, part_rows, third), bf16),
+            pltpu.VMEM((2, AXES, part_rows, third), bf16),
+            pltpu.VMEM((8, third), f32),
+            pltpu.VMEM((devices, 8, 128), f32),
+            pltpu.SemaphoreType.DMA((8, AXES)),
+            pltpu.SemaphoreType.DMA((8, AXES)),
+            pltpu.SemaphoreType.DMA((AXES, SLOTS)),
+            pltpu.SemaphoreType.DMA((7, AXES, CHUNKS)),
+            pltpu.SemaphoreType.DMA((2, AXES)),
+            pltpu.SemaphoreType.DMA((2, AXES)),
+            pltpu.SemaphoreType.DMA((devices,)),
+            pltpu.SemaphoreType.DMA((devices,)),
+            pltpu.SemaphoreType.DMA((AXES, CHUNKS)),
+        ],
+        compiler_params=pltpu.CompilerParams(has_side_effects=True, vmem_limit_bytes=60 * 1024 * 1024),
+        name='reduce',
+    )(local_grads)
+    return g, scale[0, 0]
+
+
 def solution(mesh):
     dev_count = mesh.shape['dp']
 
@@ -58,9 +287,7 @@
         shard_rows = master.shape[0]
         model_width = master.shape[1]
         total_rows = shard_rows * dev_count
-        grad_shard = lax.psum_scatter(local_grads[0].astype(jnp.float32), 'dp', scatter_dimension=0, tiled=True) / dev_count
-        square_sum = lax.psum(jnp.sum(grad_shard * grad_shard), 'dp')
-        clip_scale = jnp.minimum(1.0, 1.0 / (jnp.sqrt(square_sum) + 1e-6))
+        grad_shard, clip_scale = reduce_scatter(local_grads, dev_count)
         row_ids = lax.axis_index('dp') * shard_rows + lax.iota(jnp.int32, shard_rows)
         lr_factor, decay_rate = row_rules(row_ids, model_width, total_rows)
         new_master, new_first, new_second = adam_rows(grad_shard, master, mom_first, mom_second, clip_scale, learn_rate, lr_factor, decay_rate)

time: 805 us -> 589 us (0.73)
  waiting for transfers between devices: 653 us -> 185 us
  Pallas kernels: 0 us -> 337 us
  other arithmetic: 70.1 us -> 16.6 us
  blocking collectives: 32 us -> 0 us
    unnamed x3 -> x1, waiting for transfers between devices: 466 us -> 0.02 us
    pallas_call x0 -> x1, Pallas kernels: none -> 337 us  [reduce_scatter(): pl.pallas_call(reduce_kernel, out_shape=(jax.ShapeDtypeStruct((rows, widt...]
    convert_element_type x1 -> x0, other arithmetic: 49.8 us -> none  [device_step(): local_grads[0].astype(jnp.float32)]
    psum x1 -> x0, blocking collectives: 32 us -> none  [device_step(): square_sum = lax.psum(jnp.sum(grad_shard * grad_shard), 'dp')]
    unnamed x3 -> x1, local copies, waits for them, and re-layouts: 34.3 us -> 34.3 us
  transfers between devices with their start and end apart: 2 -> 1, of which waited for: 2 -> 1; matrix products, arithmetic and copies ran while one was open for 0% -> 0% of each run, Pallas kernels for 0% -> 0%
where the time goes in v1:
time: 589 us
  Pallas kernels  337 us (57%)
  waiting for transfers between devices  185 us (31%)
  local copies, waits for them, and re-layouts  35.6 us (6%)
  other arithmetic  16.6 us (3%)
  between operations  14.7 us (2%)
    pallas_call x1, Pallas kernels, reduce_scatter(): pl.pallas_call(reduce_kernel, out_shape=(jax.ShapeDtypeStruct((rows, widt...  337 us
    all_gather x1, waiting for transfers between devices, device_step(): lax.all_gather(new_master.astype(jnp.bfloat16), 'dp', axis=0, tiled=True)  185 us
    unnamed x1, local copies, waits for them, and re-layouts  34.3 us
    convert_element_type x1, other arithmetic, device_step(): new_master.astype(jnp.bfloat16)  15.6 us
  transfers between devices with their start and end apart: 1, of which 1 were waited for; matrix products, arithmetic and copies ran while one was open for 0% of the time, Pallas kernels for 0%

profile of v1, /device:TPU:0, one launch (start us, length us, event | category | flops | bytes accessed | tf_op | source)
XLA Modules:
  0.0 589.2 jit_solution(4035855630064727152)
XLA Ops:
  7.2 0.0 all-gather.2.cloned.1.call-start
  7.2 0.8 convert_reduce_fusion
  8.1 0.2 compare_reduce_fusion.9
  8.9 336.7 %reduce.21 = (f32[2048,768]{1,0:T(8,128)}, f32[8,128]{1,0:T(8,128)}, bf16[8,3,2048,256]{3,2,1,0:T(8,128)(2,1)}) custom-call(bf16[1,32768,768]{2,1,0:T(8,128)(2,1)} %grads.1), custom_call_target="tpu_custom_call" | custom-call | tf_op jit(solution)/shard_map/reduce/pallas_call | solution.py:253
  345.7 1.3 slice.3
  347.0 15.6 %fusion = (bf16[2048,768]{1,0:T(8,128)(2,1)}, f32[2048,768]{1,0:T(8,128)}, f32[2048,768]{1,0:T(8,128)}, f32[2048,768]{1,0:T(8,128)}) fusion(f32[2048,768]{1,0:T(8,128)} %param.9, f32[2048]{0:T(1024)S(1)} %get-tuple-element.25, f32[2048]{0:T(1024)S(1)} %get-tuple-element.24, f32[2048,768]{1,0:T(8,128)} %get-tuple-element.6, f32[]{:T(128)} %bitcast.2, ...), kind=kLoop, calls=%fused_computation.29 | loop fusion | flops 26738688 | bytes 47202308 | tf_op jit(solution)/shard_map/convert_element_type | solution.py:294
  362.6 0.0 all-gather.2.cloned.1.call-update
  362.6 185.5 %all-gather.2.cloned.1.call-done = bf16[32768,768]{1,0:T(8,128)(2,1)} async-done(((bf16[2048,768]{1,0:T(8,128)(2,1)}), bf16[32768,768]{1,0:T(8,128)(2,1)}) %all-gather.2.cloned.1.call-update) | async-done | bytes 50331664 | tf_op jit(solution)/shard_map/all_gather | solution.py:294
  548.0 34.3 %copy.14 = bf16[32768,768]{1,0:T(8,128)(2,1)} copy(bf16[32768,768]{1,0:T(8,128)(2,1)} %all-gather.2.cloned.1.call-done) | data formatting | bytes 100663296
  (4 shorter events, 0.1 us)
Async XLA Ops:
  7.2 540.9 %all-gather.2.cloned.1.call-start = ((), (), s32[]{:S(2)}) async-start(), calls=%async_computation | async-start | bytes 53477376 | tf_op jit(solution)/shard_map/all_gather | solution.py:294
Sparse Core Ops, SparseCore 0:
  362.7 185.2 all-gather.1

commit v2 on v1

--- a/solution.py
+++ b/solution.py
@@ -15,6 +15,7 @@
 AXES = 3
 CHUNKS = 4
 SLOTS = 3
+PIECE_ROWS = 256
 MESH = pl.DeviceIdType.MESH
 
 
@@ -40,26 +41,6 @@
     return run_starts, lr_values, decay_values
 
 
-def row_rules(row_ids, model_width, total_rows):
-    run_starts, lr_values, decay_values = layout_runs(model_width, total_rows)
-    later_starts = jnp.asarray(run_starts[1:], jnp.int32)
-    run_index = jnp.sum((row_ids[:, None] >= later_starts[None, :]).astype(jnp.int32), axis=1)
-    lr_factor = jnp.asarray(lr_values, jnp.float32)[run_index]
-    decay_rate = jnp.asarray(decay_values, jnp.float32)[run_index]
-    return lr_factor[:, None], decay_rate[:, None]
-
-
-def adam_rows(grad_rows, master_rows, first_rows, second_rows, clip_scale, learn_rate, lr_factor, decay_rate):
-    clipped = grad_rows * clip_scale
-    new_first = 0.9 * first_rows + 0.1 * clipped
-    new_second = 0.99 * second_rows + 0.01 * (clipped * clipped)
-    first_hat = new_first / (1.0 - 0.9 ** ADAM_STEP)
-    second_hat = new_second / (1.0 - 0.99 ** ADAM_STEP)
-    step_size = learn_rate * lr_factor
-    new_master = master_rows - step_size * (first_hat / (jnp.sqrt(second_hat) + 1e-8) + decay_rate * master_rows)
-    return new_master, new_first, new_second
-
-
 def bit_flip(index, mask):
     flipped = index
     for bit in range(4):
@@ -67,14 +48,6 @@
         if mask & step:
             flipped = flipped + step - 2 * step * ((index // step) % 2)
     return flipped
-
-
-def dest_mask(e, k):
-    mask = 0
-    for place in range(AXES):
-        if e >> (2 - place) & 1:
-            mask |= 1 << ((k + place) % AXES)
-    return mask
 
 
 def reduce_kernel(grads, g_out, c_out, pairs, landed, stage, own_buf, pair_buf, part_buf, norm_buf,
@@ -277,21 +250,267 @@
         compiler_params=pltpu.CompilerParams(has_side_effects=True, vmem_limit_bytes=60 * 1024 * 1024),
         name='reduce',
     )(local_grads)
-    return g, scale[0, 0]
+    return g, scale
+
+
+def update_gather_kernel(grad, master, first, second, scale, rate, working, new_master, new_first, new_second,
+                         in_buf, out_buf, in_sem, out_sem, own_ssem, own_rsem, fwd_ssem, fwd_rsem, pair_ssem, pair_rsem):
+    me = lax.axis_index('dp')
+    partner = bit_flip(me, 1)
+    rows, width = grad.shape
+    third = width // AXES
+    total_rows = working.shape[0]
+    pieces = rows // PIECE_ROWS
+    inputs = (grad, master, first, second)
+    outputs = (new_master, new_first, new_second)
+
+    def piece_at(owner, i, cols):
+        return working.at[pl.ds(pl.multiple_of(owner * rows + i * PIECE_ROWS, PIECE_ROWS), PIECE_ROWS), cols]
+
+    def send(owner, i, cols, ssem, rsem, target):
+        ref = piece_at(owner, i, cols)
+        return pltpu.make_async_remote_copy(src_ref=ref, dst_ref=ref, send_sem=ssem, recv_sem=rsem,
+                                            device_id=(target,), device_id_type=MESH)
+
+    every = pl.ds(0, width)
+
+    def cols_of(k):
+        return pl.ds((k % AXES) * third, third)
+
+    def chip_flip(*axes):
+        mask = 0
+        for axis in axes:
+            mask ^= 2 << (axis % AXES)
+        return bit_flip(me, mask)
+
+    def load(i, n):
+        return pltpu.make_async_copy(inputs[n].at[pl.ds(pl.multiple_of(i * PIECE_ROWS, PIECE_ROWS), PIECE_ROWS)], in_buf.at[i % 2, n], in_sem.at[i % 2, n])
+
+    def store(i, n):
+        return pltpu.make_async_copy(out_buf.at[i % 2, n], outputs[n].at[pl.ds(pl.multiple_of(i * PIECE_ROWS, PIECE_ROWS), PIECE_ROWS)], out_sem.at[i % 2, n])
+
+    def own_send(i, axis):
+        return send(me, i, every, own_ssem.at[axis, i], own_rsem.at[axis, i], chip_flip(axis))
+
+    def own_recv(i, axis):
+        return send(chip_flip(axis), i, every, own_ssem.at[axis, i], own_rsem.at[axis, i], chip_flip(axis))
+
+    hops = (((0,), 1), ((0,), 2), ((1,), 2), ((0, 1), 2))
+
+    def fwd_send(i, kind, k):
+        source, axis = hops[kind]
+        return send(chip_flip(*[k + a for a in source]), i, cols_of(k), fwd_ssem.at[kind, k, i], fwd_rsem.at[kind, k, i], chip_flip(k + axis))
+
+    def fwd_recv(i, kind, k):
+        source, axis = hops[kind]
+        return send(chip_flip(*[k + a for a in source], k + axis), i, cols_of(k), fwd_ssem.at[kind, k, i], fwd_rsem.at[kind, k, i], chip_flip(k + axis))
+
+    def pair_own(i, parity=0):
+        owner = me if parity == 0 else partner
+        return send(owner, i, every, pair_ssem.at[0, i], pair_rsem.at[0, i], partner)
+
+    def pair_axis(i, axis, parity=0):
+        owner = chip_flip(axis)
+        owner = owner if parity == 0 else bit_flip(owner, 1)
+        return send(owner, i, every, pair_ssem.at[1 + axis, i], pair_rsem.at[1 + axis, i], partner)
+
+    def pair_fwd(i, kind, k, parity=0):
+        source, axis = hops[kind]
+        owner = chip_flip(*[k + a for a in source], k + axis)
+        owner = owner if parity == 0 else bit_flip(owner, 1)
+        slot = 4 + kind * AXES + k
+        return send(owner, i, cols_of(k), pair_ssem.at[slot, i], pair_rsem.at[slot, i], partner)
+
+    clip = scale[0, 0]
+    learn_rate = rate[0]
+    run_starts, lr_values, decay_values = layout_runs(width, total_rows)
+    first_norm = 1.0 / (1.0 - 0.9 ** ADAM_STEP)
+    second_norm = 1.0 / (1.0 - 0.99 ** ADAM_STEP)
+
+    for n in range(4):
+        load(0, n).start()
+
+    def own_piece(i, carry):
+        @pl.when(i + 1 < pieces)
+        def _():
+            for n in range(4):
+                load(i + 1, n).start()
+        for n in range(4):
+            load(i, n).wait()
+
+        @pl.when(i >= 2)
+        def _():
+            for n in range(3):
+                store(i - 2, n).wait()
+        slot = i % 2
+        group = 16
+
+        def group_step(r, carry):
+            lo = pl.multiple_of(r * group, group)
+            here = pl.ds(lo, group)
+            start = me * rows + i * PIECE_ROWS + lo
+            row_ids = start + lax.broadcasted_iota(jnp.int32, (group, 128), 0)
+            factor = jnp.full((group, 128), lr_values[0], jnp.float32)
+            decay = jnp.full((group, 128), decay_values[0], jnp.float32)
+            for r_start, r_lr, r_decay in zip(run_starts[1:], lr_values[1:], decay_values[1:]):
+                past = row_ids >= r_start
+                factor = jnp.where(past, r_lr, factor)
+                decay = jnp.where(past, r_decay, decay)
+            step_size = learn_rate * factor
+            for tile in range(width // 128):
+                at = pl.ds(tile * 128, 128)
+                clipped = in_buf[slot, 0, here, at] * clip
+                weights = in_buf[slot, 1, here, at]
+                moment = 0.9 * in_buf[slot, 2, here, at] + 0.1 * clipped
+                square = 0.99 * in_buf[slot, 3, here, at] + 0.01 * (clipped * clipped)
+                moved = weights - step_size * ((moment * first_norm) / (jnp.sqrt(square * second_norm) + 1e-8) + decay * weights)
+                out_buf[slot, 0, here, at] = moved
+                out_buf[slot, 1, here, at] = moment
+                out_buf[slot, 2, here, at] = square
+                working[pl.ds(pl.multiple_of(start, group), group), at] = moved.astype(jnp.bfloat16)
+            return carry
+
+        lax.fori_loop(0, PIECE_ROWS // group, group_step, 0)
+        for axis in range(AXES):
+            own_send(i, axis).start()
+        pair_own(i).start()
+        for n in range(3):
+            store(i, n).start()
+        return carry
+
+    def neighbour_piece(i, carry):
+        for axis in range(AXES):
+            own_recv(i, axis).wait_recv()
+            pair_axis(i, axis).start()
+        for kind in range(3):
+            for k in range(AXES):
+                fwd_send(i, kind, k).start()
+        return carry
+
+    def far_piece(i, carry):
+        for k in range(AXES):
+            fwd_recv(i, 0, k).wait_recv()
+            fwd_send(i, 3, k).start()
+            pair_fwd(i, 0, k).start()
+        for kind in (1, 2):
+            for k in range(AXES):
+                fwd_recv(i, kind, k).wait_recv()
+                pair_fwd(i, kind, k).start()
+        return carry
+
+    def last_piece(i, carry):
+        for k in range(AXES):
+            fwd_recv(i, 3, k).wait_recv()
+            pair_fwd(i, 3, k).start()
+        return carry
+
+    def drain(i, carry):
+        for axis in range(AXES):
+            own_send(i, axis).wait_send()
+            pair_axis(i, axis).wait_send()
+            pair_axis(i, axis, 1).wait_recv()
+        pair_own(i).wait_send()
+        pair_own(i, 1).wait_recv()
+        for kind in range(4):
+            for k in range(AXES):
+                fwd_send(i, kind, k).wait_send()
+                pair_fwd(i, kind, k).wait_send()
+                pair_fwd(i, kind, k, 1).wait_recv()
+        return carry
+
+    lax.fori_loop(0, pieces, own_piece, 0)
+    lax.fori_loop(0, pieces, neighbour_piece, 0)
+    for i in (pieces - 2, pieces - 1):
+        for n in range(3):
+            store(i, n).wait()
+    lax.fori_loop(0, pieces, far_piece, 0)
+    lax.fori_loop(0, pieces, last_piece, 0)
+    lax.fori_loop(0, pieces, drain, 0)
+
+
+def write_kernel(working, new_master, new_first, new_second, working_out, master_out, first_out, second_out,
+                 buf, working_sem, in_sem, out_sem):
+    pairs = ((new_master, master_out), (new_first, first_out), (new_second, second_out))
+    slots = buf.shape[0]
+    piece = buf.shape[1]
+    per = master_out.shape[0] // piece
+    steps = 3 * per
+
+    def load(s):
+        return pltpu.make_async_copy(pairs[s // per][0].at[pl.ds(s % per * piece, piece)], buf.at[s % slots], in_sem.at[s % slots])
+
+    def store(s):
+        return pltpu.make_async_copy(buf.at[s % slots], pairs[s // per][1].at[pl.ds(s % per * piece, piece)], out_sem.at[s % slots])
+
+    stripes = working_sem.shape[0]
+    stripe = working.shape[0] // stripes
+
+    def put(n):
+        here = pl.ds(n * stripe, stripe)
+        return pltpu.make_async_copy(working.at[here], working_out.at[here], working_sem.at[n])
+
+    for s in range(slots):
+        load(s).start()
+    for n in range(stripes):
+        put(n).start()
+    for s in range(steps):
+        load(s).wait()
+        store(s).start()
+        if s + 1 >= slots and s + 1 < steps:
+            store(s + 1 - slots).wait()
+            load(s + 1).start()
+    for s in range(max(steps - slots, 0), steps):
+        store(s).wait()
+    for n in range(stripes):
+        put(n).wait()
+
+
+def update_gather(grad, master, first, second, scale, rate, devices):
+    rows, width = grad.shape
+    any_spec = pl.BlockSpec(memory_space=pltpu.HBM)
+    vmem_spec = pl.BlockSpec(memory_space=pltpu.VMEM)
+    f32, bf16 = jnp.float32, jnp.bfloat16
+    pieces = rows // PIECE_ROWS
+    shard = pltpu.HBM((rows, width), f32)
+    dma = pltpu.SemaphoreType.DMA
+    working, *news = pl.pallas_call(
+        update_gather_kernel,
+        out_shape=(pltpu.VMEM((devices * rows, width), bf16), shard, shard, shard),
+        in_specs=[any_spec] * 4 + [vmem_spec, pl.BlockSpec(memory_space=pltpu.SMEM)],
+        out_specs=(vmem_spec, any_spec, any_spec, any_spec),
+        scratch_shapes=[
+            pltpu.VMEM((2, 4, PIECE_ROWS, width), f32),
+            pltpu.VMEM((2, 3, PIECE_ROWS, width), f32),
+            dma((2, 4)),
+            dma((2, 3)),
+            dma((AXES, pieces)),
+            dma((AXES, pieces)),
+            dma((4, AXES, pieces)),
+            dma((4, AXES, pieces)),
+            dma((16, pieces)),
+            dma((16, pieces)),
+        ],
+        compiler_params=pltpu.CompilerParams(has_side_effects=True, vmem_limit_bytes=12 * 1024 * 1024),
+        name='gather',
+    )(grad, master, first, second, scale, rate.reshape(1))
+    working_shape = pltpu.HBM((devices * rows, width), bf16)
+    return pl.pallas_call(
+        write_kernel,
+        out_shape=(working_shape, shard, shard, shard),
+        in_specs=[vmem_spec, any_spec, any_spec, any_spec],
+        out_specs=(any_spec,) * 4,
+        scratch_shapes=[pltpu.VMEM((6, rows // 4, width), f32), dma((16,)), dma((6,)), dma((6,))],
+        compiler_params=pltpu.CompilerParams(vmem_limit_bytes=12 * 1024 * 1024),
+        name='write',
+    )(pltpu.with_memory_space_constraint(working, pltpu.VMEM), *news)
 
 
 def solution(mesh):
     dev_count = mesh.shape['dp']
 
     def device_step(local_grads, master, mom_first, mom_second, learn_rate):
-        shard_rows = master.shape[0]
-        model_width = master.shape[1]
-        total_rows = shard_rows * dev_count
         grad_shard, clip_scale = reduce_scatter(local_grads, dev_count)
-        row_ids = lax.axis_index('dp') * shard_rows + lax.iota(jnp.int32, shard_rows)
-        lr_factor, decay_rate = row_rules(row_ids, model_width, total_rows)
-        new_master, new_first, new_second = adam_rows(grad_shard, master, mom_first, mom_second, clip_scale, learn_rate, lr_factor, decay_rate)
-        working = lax.all_gather(new_master.astype(jnp.bfloat16), 'dp', axis=0, tiled=True)
+        working, new_master, new_first, new_second = update_gather(grad_shard, master, mom_first, mom_second, clip_scale, learn_rate, dev_count)
         return new_master, new_first, new_second, working
 
     return jax.shard_map(device_step, mesh=mesh, in_specs=(P('dp', None, None), P('dp', None), P('dp', None), P('dp', None), P()), out_specs=(P('dp', None), P('dp', None), P('dp', None), P(None, None)), check_vma=False)

time: 589 us -> 543 us (0.922)
  Pallas kernels: 337 us -> 542 us
  waiting for transfers between devices: 185 us -> 0 us
  local copies, waits for them, and re-layouts: 35.6 us -> 0 us
  other arithmetic: 16.6 us -> 0 us
  between operations: 14.7 us -> 1.29 us
    pallas_call x0 -> x2, Pallas kernels: none -> 205 us  [the longest x1 171 us: update_gather(): pl.pallas_call(update_gather_kernel, out_shape=(pltpu.VMEM((devices * row...]
    all_gather x1 -> x0, waiting for transfers between devices: 185 us -> none  [device_step(): lax.all_gather(new_master.astype(jnp.bfloat16), 'dp', axis=0, tiled=True)]
    unnamed x1 -> x0, local copies, waits for them, and re-layouts: 34.3 us -> none
    convert_element_type x1 -> x0, other arithmetic: 15.6 us -> none  [device_step(): new_master.astype(jnp.bfloat16)]
  transfers between devices with their start and end apart: 1 -> 0, of which waited for: 1 -> 0; matrix products, arithmetic and copies ran while one was open for 0% -> 0% of each run, Pallas kernels for 0% -> 0%
where the time goes in v2:
time: 543 us
  Pallas kernels  542 us (100%)
    pallas_call x1, Pallas kernels, reduce_scatter(): pl.pallas_call(reduce_kernel, out_shape=(jax.ShapeDtypeStruct((rows, widt...  337 us
    pallas_call x1, Pallas kernels, update_gather(): pl.pallas_call(update_gather_kernel, out_shape=(pltpu.VMEM((devices * row...  171 us
    pallas_call x1, Pallas kernels, update_gather(): pl.pallas_call(write_kernel, out_shape=(working_shape, shard, shard, shar...  33.5 us

profile of v2, /device:TPU:0, one launch (start us, length us, event | category | flops | bytes accessed | tf_op | source)
XLA Modules:
  0.0 542.9 jit_solution(15969552591137438588)
XLA Ops:
  1.3 336.7 %reduce.1 = (f32[2048,768]{1,0:T(8,128)}, f32[8,128]{1,0:T(8,128)}, bf16[8,3,2048,256]{3,2,1,0:T(8,128)(2,1)}) custom-call(bf16[1,32768,768]{2,1,0:T(8,128)(2,1)} %grads.1), custom_call_target="tpu_custom_call" | custom-call | tf_op jit(solution)/shard_map/reduce/pallas_call | solution.py:226
  338.0 171.5 %gather.1 = (bf16[32768,768]{1,0:T(8,128)(2,1)S(1)}, f32[2048,768]{1,0:T(8,128)}, f32[2048,768]{1,0:T(8,128)}, f32[2048,768]{1,0:T(8,128)}) custom-call(f32[2048,768]{1,0:T(8,128)} %get-tuple-element.14.grad, f32[2048,768]{1,0:T(8,128)} %master.1, f32[2048,768]{1,0:T(8,128)} %first.1, f32[2048,768]{1,0:T(8,128)} %second.1, ...), custom_call_target="tpu_custom_call" | custom-call | tf_op jit(solution)/shard_map/gather/pallas_call | solution.py:476
  509.5 33.5 %write.1 = (bf16[32768,768]{1,0:T(8,128)(2,1)}, f32[2048,768]{1,0:T(8,128)}, f32[2048,768]{1,0:T(8,128)}, f32[2048,768]{1,0:T(8,128)}) custom-call(bf16[32768,768]{1,0:T(8,128)(2,1)S(1)} %get-tuple-element.16.working, f32[2048,768]{1,0:T(8,128)} %get-tuple-element.17.new_master, f32[2048,768]{1,0:T(8,128)} %get-tuple-element.18.new_first, ...), custom_call_target="tpu_custom_call" | custom-call | tf_op jit(solution)/shard_map/write/pallas_call | solution.py:497

commit v3 on v2

--- a/solution.py
+++ b/solution.py
@@ -15,7 +15,10 @@
 AXES = 3
 CHUNKS = 4
 SLOTS = 3
+AHEAD = 4
 PIECE_ROWS = 256
+LOAD_ROWS = 64
+LOADS = 3
 MESH = pl.DeviceIdType.MESH
 
 
@@ -61,7 +64,6 @@
     devices = norm_buf.shape[0]
 
     def unit_row(j, k, parity):
-        row = 0
         flip = chip
         e = 7 - j
         for place in range(AXES):
@@ -69,14 +71,16 @@
             want = (e // (1 << (2 - place))) % 2
             bit = (chip // step) % 2
             flip = flip + want * (step - 2 * step * bit)
-        return (2 * flip + parity) * rows + row
-
-    def pair_copy(j, k):
+        return (2 * flip + parity) * rows
+
+    def pair_copy(s, k):
+        j, i = s // CHUNKS, s % CHUNKS
+        row = pl.multiple_of(unit_row(j, k, 1 - core) + i * part_rows, part_rows)
         return pltpu.make_async_remote_copy(
-            src_ref=grads.at[0, pl.ds(pl.multiple_of(unit_row(j, k, 1 - core), rows), rows), pl.ds(k * third, third)],
-            dst_ref=pairs.at[j, k],
-            send_sem=pair_ssem.at[j, k],
-            recv_sem=pair_rsem.at[j, k],
+            src_ref=grads.at[0, pl.ds(row, part_rows), pl.ds(k * third, third)],
+            dst_ref=pairs.at[j, k, pl.ds(pl.multiple_of(i * part_rows, part_rows), part_rows)],
+            send_sem=pair_ssem.at[j, k, i],
+            recv_sem=pair_rsem.at[j, k, i],
             device_id=(partner,),
             device_id_type=MESH)
 
@@ -100,27 +104,45 @@
             device_id=(bit_flip(me, 2 << axis),),
             device_id_type=MESH)
 
-    def start_loads(s):
-        for k in range(AXES):
-            @pl.when(s % CHUNKS == 0)
-            def _():
-                pair_copy(s // CHUNKS, k).wait_recv()
+    total_steps = 8 * CHUNKS
+
+    def start_pairs(s):
+        for k in range(AXES):
+            pair_copy(s, k).start()
+
+    def start_own(s):
+        for k in range(AXES):
             own_load(s, k).start()
+
+    def start_pair_loads(s):
+        for k in range(AXES):
+            pair_copy(s, k).wait_recv()
             pair_load(s, k).start()
 
-    for j in range(8):
-        for k in range(AXES):
-            pair_copy(j, k).start()
-
-    total_steps = 8 * CHUNKS
-    start_loads(0)
+    barrier = pltpu.get_barrier_semaphore()
+    for d in range(1, devices):
+        pl.semaphore_signal(barrier, inc=1, device_id=((me + d) % devices,), device_id_type=MESH)
+    start_own(0)
+    pl.semaphore_wait(barrier, devices - 1)
+    for s in range(AHEAD):
+        start_pairs(s)
+    start_pair_loads(0)
 
     def step(s, phase):
         j, i = s // CHUNKS, s % CHUNKS
 
+        @pl.when(s + AHEAD < total_steps)
+        def _():
+            start_pairs(s + AHEAD)
+
         @pl.when(s + 1 < total_steps)
         def _():
-            start_loads(s + 1)
+            start_own(s + 1)
+
+        def load_next():
+            @pl.when(s + 1 < total_steps)
+            def _():
+                start_pair_loads(s + 1)
 
         if phase == 1:
             sources = []
@@ -159,13 +181,13 @@
                 lax.fori_loop(0, part_rows // group, add_rows, 0)
             else:
                 part_buf[...] += lax.fori_loop(0, part_rows // group, add_rows, jnp.zeros((8, third), jnp.float32))
-        for k in range(AXES):
             if phase < 4:
                 piece_copy(j, i, k, slot, (k + phase - 1) % AXES).start()
             else:
                 pltpu.make_async_copy(
                     landed.at[0, k, pl.ds(base, part_rows)],
                     g_out.at[pl.ds(base, part_rows), pl.ds(k * third, third)], g_sem.at[k, i]).start()
+        load_next()
 
     part_buf[...] = jnp.zeros_like(part_buf)
     for phase, lo, hi in ((1, 0, 4), (2, 4, 6), (3, 6, 7), (4, 7, 8)):
@@ -201,9 +223,12 @@
     for last in range(SLOTS):
         for k in range(AXES):
             piece_copy(0, 0, k, last, 0).wait_send()
-    for j in range(8):
-        for k in range(AXES):
-            pair_copy(j, k).wait_send()
+    def drain_pair(s, carry):
+        for k in range(AXES):
+            pair_copy(s, k).wait_send()
+        return carry
+
+    lax.fori_loop(0, total_steps, drain_pair, 0)
     for i in range(CHUNKS):
         for k in range(AXES):
             pltpu.make_async_copy(
@@ -237,8 +262,8 @@
             pltpu.VMEM((2, AXES, part_rows, third), bf16),
             pltpu.VMEM((8, third), f32),
             pltpu.VMEM((devices, 8, 128), f32),
-            pltpu.SemaphoreType.DMA((8, AXES)),
-            pltpu.SemaphoreType.DMA((8, AXES)),
+            pltpu.SemaphoreType.DMA((8, AXES, CHUNKS)),
+            pltpu.SemaphoreType.DMA((8, AXES, CHUNKS)),
             pltpu.SemaphoreType.DMA((AXES, SLOTS)),
             pltpu.SemaphoreType.DMA((7, AXES, CHUNKS)),
             pltpu.SemaphoreType.DMA((2, AXES)),
@@ -247,7 +272,7 @@
             pltpu.SemaphoreType.DMA((devices,)),
             pltpu.SemaphoreType.DMA((AXES, CHUNKS)),
         ],
-        compiler_params=pltpu.CompilerParams(has_side_effects=True, vmem_limit_bytes=60 * 1024 * 1024),
+        compiler_params=pltpu.CompilerParams(has_side_effects=True, vmem_limit_bytes=60 * 1024 * 1024, collective_id=0),
         name='reduce',
     )(local_grads)
     return g, scale
@@ -262,7 +287,6 @@
     total_rows = working.shape[0]
     pieces = rows // PIECE_ROWS
     inputs = (grad, master, first, second)
-    outputs = (new_master, new_first, new_second)
 
     def piece_at(owner, i, cols):
         return working.at[pl.ds(pl.multiple_of(owner * rows + i * PIECE_ROWS, PIECE_ROWS), PIECE_ROWS), cols]
@@ -283,11 +307,13 @@
             mask ^= 2 << (axis % AXES)
         return bit_flip(me, mask)
 
-    def load(i, n):
-        return pltpu.make_async_copy(inputs[n].at[pl.ds(pl.multiple_of(i * PIECE_ROWS, PIECE_ROWS), PIECE_ROWS)], in_buf.at[i % 2, n], in_sem.at[i % 2, n])
-
-    def store(i, n):
-        return pltpu.make_async_copy(out_buf.at[i % 2, n], outputs[n].at[pl.ds(pl.multiple_of(i * PIECE_ROWS, PIECE_ROWS), PIECE_ROWS)], out_sem.at[i % 2, n])
+    def load(t, n):
+        here = pl.ds(pl.multiple_of(t * LOAD_ROWS, LOAD_ROWS), LOAD_ROWS)
+        return pltpu.make_async_copy(inputs[n].at[here], in_buf.at[t % LOADS, n], in_sem.at[t % LOADS, n])
+
+    def store(t):
+        here = pl.ds(pl.multiple_of(t * LOAD_ROWS, LOAD_ROWS), LOAD_ROWS)
+        return pltpu.make_async_copy(out_buf.at[t % 2], new_second.at[here], out_sem.at[t % 2])
 
     def own_send(i, axis):
         return send(me, i, every, own_ssem.at[axis, i], own_rsem.at[axis, i], chip_flip(axis))
@@ -327,28 +353,32 @@
     first_norm = 1.0 / (1.0 - 0.9 ** ADAM_STEP)
     second_norm = 1.0 / (1.0 - 0.99 ** ADAM_STEP)
 
-    for n in range(4):
-        load(0, n).start()
-
-    def own_piece(i, carry):
-        @pl.when(i + 1 < pieces)
+    steps = rows // LOAD_ROWS
+    barrier = pltpu.get_barrier_semaphore()
+    peers = [partner] + [chip_flip(axis) for axis in range(AXES)]
+    for peer in peers:
+        pl.semaphore_signal(barrier, inc=1, device_id=(peer,), device_id_type=MESH)
+    for t in range(LOADS):
+        for n in range(4):
+            load(t, n).start()
+    pl.semaphore_wait(barrier, len(peers))
+
+    def update_rows(t, carry):
+        for n in range(4):
+            load(t, n).wait()
+
+        @pl.when(t >= 2)
         def _():
-            for n in range(4):
-                load(i + 1, n).start()
-        for n in range(4):
-            load(i, n).wait()
-
-        @pl.when(i >= 2)
-        def _():
-            for n in range(3):
-                store(i - 2, n).wait()
-        slot = i % 2
+            store(t - 2).wait()
+        slot = t % LOADS
+        out_slot = t % 2
         group = 16
 
         def group_step(r, carry):
             lo = pl.multiple_of(r * group, group)
             here = pl.ds(lo, group)
-            start = me * rows + i * PIECE_ROWS + lo
+            row = pl.multiple_of(t * LOAD_ROWS + lo, group)
+            start = me * rows + row
             row_ids = start + lax.broadcasted_iota(jnp.int32, (group, 128), 0)
             factor = jnp.full((group, 128), lr_values[0], jnp.float32)
             decay = jnp.full((group, 128), decay_values[0], jnp.float32)
@@ -364,18 +394,27 @@
                 moment = 0.9 * in_buf[slot, 2, here, at] + 0.1 * clipped
                 square = 0.99 * in_buf[slot, 3, here, at] + 0.01 * (clipped * clipped)
                 moved = weights - step_size * ((moment * first_norm) / (jnp.sqrt(square * second_norm) + 1e-8) + decay * weights)
-                out_buf[slot, 0, here, at] = moved
-                out_buf[slot, 1, here, at] = moment
-                out_buf[slot, 2, here, at] = square
+                new_master[pl.ds(row, group), at] = moved
+                new_first[pl.ds(row, group), at] = moment
+                out_buf[out_slot, here, at] = square
                 working[pl.ds(pl.multiple_of(start, group), group), at] = moved.astype(jnp.bfloat16)
             return carry
 
-        lax.fori_loop(0, PIECE_ROWS // group, group_step, 0)
+        lax.fori_loop(0, LOAD_ROWS // group, group_step, 0)
+        store(t).start()
+
+        @pl.when(t + LOADS < steps)
+        def _():
+            for n in range(4):
+                load(t + LOADS, n).start()
+        return carry
+
+    def own_piece(i, carry):
+        per = PIECE_ROWS // LOAD_ROWS
+        lax.fori_loop(i * per, (i + 1) * per, update_rows, 0)
         for axis in range(AXES):
             own_send(i, axis).start()
         pair_own(i).start()
-        for n in range(3):
-            store(i, n).start()
         return carry
 
     def neighbour_piece(i, carry):
@@ -420,49 +459,46 @@
 
     lax.fori_loop(0, pieces, own_piece, 0)
     lax.fori_loop(0, pieces, neighbour_piece, 0)
-    for i in (pieces - 2, pieces - 1):
-        for n in range(3):
-            store(i, n).wait()
+    for t in (steps - 2, steps - 1):
+        store(t).wait()
     lax.fori_loop(0, pieces, far_piece, 0)
     lax.fori_loop(0, pieces, last_piece, 0)
     lax.fori_loop(0, pieces, drain, 0)
 
 
 def write_kernel(working, new_master, new_first, new_second, working_out, master_out, first_out, second_out,
-                 buf, working_sem, in_sem, out_sem):
-    pairs = ((new_master, master_out), (new_first, first_out), (new_second, second_out))
-    slots = buf.shape[0]
-    piece = buf.shape[1]
-    per = master_out.shape[0] // piece
-    steps = 3 * per
+                 buf, put_sem, in_sem, out_sem):
+    rows = new_second.shape[0]
+    slots, piece = buf.shape[:2]
+    steps = rows // piece
 
     def load(s):
-        return pltpu.make_async_copy(pairs[s // per][0].at[pl.ds(s % per * piece, piece)], buf.at[s % slots], in_sem.at[s % slots])
+        return pltpu.make_async_copy(new_second.at[pl.ds(s * piece, piece)], buf.at[s % slots], in_sem.at[s % slots])
 
     def store(s):
-        return pltpu.make_async_copy(buf.at[s % slots], pairs[s // per][1].at[pl.ds(s % per * piece, piece)], out_sem.at[s % slots])
-
-    stripes = working_sem.shape[0]
+        return pltpu.make_async_copy(buf.at[s % slots], second_out.at[pl.ds(s * piece, piece)], out_sem.at[s % slots])
+
+    puts = [pltpu.make_async_copy(new_master, master_out, put_sem.at[0]), pltpu.make_async_copy(new_first, first_out, put_sem.at[1])]
+    stripes = put_sem.shape[0] - 2
     stripe = working.shape[0] // stripes
-
-    def put(n):
+    for n in range(stripes):
         here = pl.ds(n * stripe, stripe)
-        return pltpu.make_async_copy(working.at[here], working_out.at[here], working_sem.at[n])
+        puts.append(pltpu.make_async_copy(working.at[here], working_out.at[here], put_sem.at[n + 2]))
 
     for s in range(slots):
         load(s).start()
-    for n in range(stripes):
-        put(n).start()
     for s in range(steps):
+        for put in puts[s * len(puts) // steps:(s + 1) * len(puts) // steps]:
+            put.start()
         load(s).wait()
         store(s).start()
         if s + 1 >= slots and s + 1 < steps:
             store(s + 1 - slots).wait()
             load(s + 1).start()
-    for s in range(max(steps - slots, 0), steps):
+    for s in range(steps - slots, steps):
         store(s).wait()
-    for n in range(stripes):
-        put(n).wait()
+    for put in puts:
+        put.wait()
 
 
 def update_gather(grad, master, first, second, scale, rate, devices):
@@ -472,17 +508,18 @@
     f32, bf16 = jnp.float32, jnp.bfloat16
     pieces = rows // PIECE_ROWS
     shard = pltpu.HBM((rows, width), f32)
+    near = pltpu.VMEM((rows, width), f32)
     dma = pltpu.SemaphoreType.DMA
-    working, *news = pl.pallas_call(
+    working, new_master, new_first, new_second = pl.pallas_call(
         update_gather_kernel,
-        out_shape=(pltpu.VMEM((devices * rows, width), bf16), shard, shard, shard),
+        out_shape=(pltpu.VMEM((devices * rows, width), bf16), near, near, shard),
         in_specs=[any_spec] * 4 + [vmem_spec, pl.BlockSpec(memory_space=pltpu.SMEM)],
-        out_specs=(vmem_spec, any_spec, any_spec, any_spec),
+        out_specs=(vmem_spec, vmem_spec, vmem_spec, any_spec),
         scratch_shapes=[
-            pltpu.VMEM((2, 4, PIECE_ROWS, width), f32),
-            pltpu.VMEM((2, 3, PIECE_ROWS, width), f32),
-            dma((2, 4)),
-            dma((2, 3)),
+            pltpu.VMEM((LOADS, 4, LOAD_ROWS, width), f32),
+            pltpu.VMEM((2, LOAD_ROWS, width), f32),
+            dma((LOADS, 4)),
+            dma((2,)),
             dma((AXES, pieces)),
             dma((AXES, pieces)),
             dma((4, AXES, pieces)),
@@ -490,19 +527,19 @@
             dma((16, pieces)),
             dma((16, pieces)),
         ],
-        compiler_params=pltpu.CompilerParams(has_side_effects=True, vmem_limit_bytes=12 * 1024 * 1024),
+        compiler_params=pltpu.CompilerParams(has_side_effects=True, vmem_limit_bytes=3 * 1024 * 1024, collective_id=1),
         name='gather',
     )(grad, master, first, second, scale, rate.reshape(1))
     working_shape = pltpu.HBM((devices * rows, width), bf16)
     return pl.pallas_call(
         write_kernel,
         out_shape=(working_shape, shard, shard, shard),
-        in_specs=[vmem_spec, any_spec, any_spec, any_spec],
+        in_specs=[vmem_spec, vmem_spec, vmem_spec, any_spec],
         out_specs=(any_spec,) * 4,
-        scratch_shapes=[pltpu.VMEM((6, rows // 4, width), f32), dma((16,)), dma((6,)), dma((6,))],
-        compiler_params=pltpu.CompilerParams(vmem_limit_bytes=12 * 1024 * 1024),
+        scratch_shapes=[pltpu.VMEM((3, rows // 8, width), f32), dma((18,)), dma((3,)), dma((3,))],
+        compiler_params=pltpu.CompilerParams(vmem_limit_bytes=3 * 1024 * 1024),
         name='write',
-    )(pltpu.with_memory_space_constraint(working, pltpu.VMEM), *news)
+    )(*[pltpu.with_memory_space_constraint(x, pltpu.VMEM) for x in (working, new_master, new_first)], new_second)
 
 
 def solution(mesh):

time: 543 us -> 528 us (0.972)
  Pallas kernels: 542 us -> 525 us
    pallas_call x1, Pallas kernels: 33.5 us -> 23.5 us  [update_gather(): pl.pallas_call(write_kernel, out_shape=(working_shape, shard, shard, shar...]
where the time goes in v3:
time: 528 us; the launch traced here: 526 us
  Pallas kernels  525 us (99%)
    pallas_call x1, Pallas kernels, reduce_scatter(): pl.pallas_call(reduce_kernel, out_shape=(jax.ShapeDtypeStruct((rows, widt...  332 us
    pallas_call x1, Pallas kernels, update_gather(): pl.pallas_call(update_gather_kernel, out_shape=(pltpu.VMEM((devices * row...  169 us
    pallas_call x1, Pallas kernels, update_gather(): pl.pallas_call(write_kernel, out_shape=(working_shape, shard, shard, shar...  23.5 us

profile of v3, /device:TPU:0, one launch (start us, length us, event | category | flops | bytes accessed | tf_op | source)
XLA Modules:
  0.0 526.3 jit_solution(368328650542650547)
XLA Ops:
  1.3 332.3 %reduce.1 = (f32[2048,768]{1,0:T(8,128)}, f32[8,128]{1,0:T(8,128)}, bf16[8,3,2048,256]{3,2,1,0:T(8,128)(2,1)}) custom-call(bf16[1,32768,768]{2,1,0:T(8,128)(2,1)} %grads.1), custom_call_target="tpu_custom_call" | custom-call | tf_op jit(solution)/shard_map/reduce/pallas_call | solution.py:251
  333.6 169.2 %gather.1 = (bf16[32768,768]{1,0:T(8,128)(2,1)S(1)}, f32[2048,768]{1,0:T(8,128)S(1)}, f32[2048,768]{1,0:T(8,128)S(1)}, f32[2048,768]{1,0:T(8,128)}) custom-call(f32[2048,768]{1,0:T(8,128)} %get-tuple-element.14.grad, f32[2048,768]{1,0:T(8,128)} %master.1, f32[2048,768]{1,0:T(8,128)} %first.1, f32[2048,768]{1,0:T(8,128)} %second.1, ...), custom_call_target="tpu_custom_call" | custom-call | tf_op jit(solution)/shard_map/gather/pallas_call | solution.py:513
  502.8 23.5 %write.1 = (bf16[32768,768]{1,0:T(8,128)(2,1)}, f32[2048,768]{1,0:T(8,128)}, f32[2048,768]{1,0:T(8,128)}, f32[2048,768]{1,0:T(8,128)}) custom-call(bf16[32768,768]{1,0:T(8,128)(2,1)S(1)} %get-tuple-element.16.working, f32[2048,768]{1,0:T(8,128)S(1)} %get-tuple-element.17.new_master, f32[2048,768]{1,0:T(8,128)S(1)} %get-tuple-element.18.new_first, ...), custom_call_target="tpu_custom_call" | custom-call | tf_op jit(solution)/shard_map/write/pallas_call | solution.py:534

commit v4 on v3

--- a/solution.py
+++ b/solution.py
@@ -13,10 +13,12 @@
 ADAM_STEP = 10
 
 AXES = 3
+UNITS = 7
 CHUNKS = 4
 SLOTS = 3
 AHEAD = 4
 PIECE_ROWS = 256
+FORWARD_ROWS = (512, 512, 512, 512)
 LOAD_ROWS = 64
 LOADS = 3
 MESH = pl.DeviceIdType.MESH
@@ -53,8 +55,8 @@
     return flipped
 
 
-def reduce_kernel(grads, g_out, c_out, pairs, landed, stage, own_buf, pair_buf, part_buf, norm_buf,
-                  pair_ssem, pair_rsem, send_sem, recv_sem, own_sem, pairl_sem, norm_ssem, norm_rsem, g_sem):
+def reduce_kernel(grads, g_out, c_out, pairs, landed, raw, stage, own_buf, pair_buf, part_buf, norm_buf,
+                  pair_ssem, pair_rsem, send_sem, recv_sem, own_sem, pairl_sem, raw_ssem, raw_rsem, norm_ssem, norm_rsem, g_sem):
     me = lax.axis_index('dp')
     chip, core = me // 2, me % 2
     partner = bit_flip(me, 1)
@@ -65,13 +67,32 @@
 
     def unit_row(j, k, parity):
         flip = chip
-        e = 7 - j
+        e = 7 - j - (j + 4) // 7
         for place in range(AXES):
             step = 1 << ((k + place) % AXES)
             want = (e // (1 << (2 - place))) % 2
             bit = (chip // step) % 2
             flip = flip + want * (step - 2 * step * bit)
         return (2 * flip + parity) * rows
+
+    def raw_copy(k, parity):
+        owner = 2 * (bit_flip(me, 2 << k) // 2) + parity
+        return pltpu.make_async_remote_copy(
+            src_ref=grads.at[0, pl.ds(pl.multiple_of(owner * rows, rows), rows), pl.ds(k * third, third)],
+            dst_ref=raw.at[k, core],
+            send_sem=raw_ssem.at[k, parity],
+            recv_sem=raw_rsem.at[k, core],
+            device_id=(owner,),
+            device_id_type=MESH)
+
+    def raw_recv(k, parity):
+        return pltpu.make_async_remote_copy(
+            src_ref=grads.at[0, pl.ds(0, rows), pl.ds(k * third, third)],
+            dst_ref=raw.at[k, parity],
+            send_sem=raw_ssem.at[k, parity],
+            recv_sem=raw_rsem.at[k, parity],
+            device_id=(partner,),
+            device_id_type=MESH)
 
     def pair_copy(s, k):
         j, i = s // CHUNKS, s % CHUNKS
@@ -104,7 +125,7 @@
             device_id=(bit_flip(me, 2 << axis),),
             device_id_type=MESH)
 
-    total_steps = 8 * CHUNKS
+    total_steps = UNITS * CHUNKS
 
     def start_pairs(s):
         for k in range(AXES):
@@ -120,10 +141,17 @@
             pair_load(s, k).start()
 
     barrier = pltpu.get_barrier_semaphore()
-    for d in range(1, devices):
-        pl.semaphore_signal(barrier, inc=1, device_id=((me + d) % devices,), device_id_type=MESH)
+    peers = [partner]
+    for k in range(AXES):
+        across = 2 * (bit_flip(me, 2 << k) // 2)
+        peers += [across, across + 1]
+    for peer in peers:
+        pl.semaphore_signal(barrier, inc=1, device_id=(peer,), device_id_type=MESH)
     start_own(0)
-    pl.semaphore_wait(barrier, devices - 1)
+    pl.semaphore_wait(barrier, len(peers))
+    for parity in range(2):
+        for k in range(AXES):
+            raw_copy(k, parity).start()
     for s in range(AHEAD):
         start_pairs(s)
     start_pair_loads(0)
@@ -147,11 +175,11 @@
         if phase == 1:
             sources = []
         elif phase == 2:
-            sources = [j - 4]
+            sources = [j - 3]
         elif phase == 3:
-            sources = [2, 4]
+            sources = [2, 3]
         else:
-            sources = [3, 5, 6]
+            sources = [4, 5]
         slot = s % SLOTS
         base = pl.multiple_of(i * part_rows, part_rows)
         for k in range(AXES):
@@ -173,6 +201,8 @@
                 if phase < 4:
                     stage[k, slot, pl.ds(lo, group)] = value
                     return carry
+                for parity in range(2):
+                    value = value + raw[k, parity, pl.ds(base + lo, group)].astype(jnp.float32)
                 value = value * (1.0 / devices)
                 landed[0, k, pl.ds(base + lo, group)] = value
                 return carry + jnp.sum((value * value).reshape(group // 8, 8, third), axis=0)
@@ -189,11 +219,22 @@
                     g_out.at[pl.ds(base, part_rows), pl.ds(k * third, third)], g_sem.at[k, i]).start()
         load_next()
 
+    def drain_pair(s, carry):
+        for k in range(AXES):
+            pair_copy(s, k).wait_send()
+        return carry
+
     part_buf[...] = jnp.zeros_like(part_buf)
-    for phase, lo, hi in ((1, 0, 4), (2, 4, 6), (3, 6, 7), (4, 7, 8)):
+    for phase, lo, hi in ((1, 0, 3), (2, 3, 5), (3, 5, 6), (4, 6, 7)):
         def run(s, carry, phase=phase):
             step(s, phase)
             return carry
+        if phase == 4:
+            lax.fori_loop(0, total_steps, drain_pair, 0)
+            for k in range(AXES):
+                for parity in range(2):
+                    raw_recv(k, parity).wait_recv()
+                    raw_copy(k, parity).wait_send()
         lax.fori_loop(lo * CHUNKS, hi * CHUNKS, run, 0)
 
     part_buf[:, :128] = part_buf[:, :128] + part_buf[:, 128:]
@@ -223,12 +264,6 @@
     for last in range(SLOTS):
         for k in range(AXES):
             piece_copy(0, 0, k, last, 0).wait_send()
-    def drain_pair(s, carry):
-        for k in range(AXES):
-            pair_copy(s, k).wait_send()
-        return carry
-
-    lax.fori_loop(0, total_steps, drain_pair, 0)
     for i in range(CHUNKS):
         for k in range(AXES):
             pltpu.make_async_copy(
@@ -252,22 +287,25 @@
         reduce_kernel,
         out_shape=(jax.ShapeDtypeStruct((rows, width), f32),
                    jax.ShapeDtypeStruct((8, 128), f32),
-                   jax.ShapeDtypeStruct((8, AXES, rows, third), bf16)),
+                   jax.ShapeDtypeStruct((UNITS, AXES, rows, third), bf16)),
         in_specs=[any_spec],
         out_specs=(any_spec, pl.BlockSpec(memory_space=pltpu.VMEM), any_spec),
         scratch_shapes=[
-            pltpu.VMEM((7, AXES, rows, third), f32),
+            pltpu.VMEM((UNITS - 1, AXES, rows, third), f32),
+            pltpu.VMEM((AXES, 2, rows, third), bf16),
             pltpu.VMEM((AXES, SLOTS, part_rows, third), f32),
             pltpu.VMEM((2, AXES, part_rows, third), bf16),
             pltpu.VMEM((2, AXES, part_rows, third), bf16),
             pltpu.VMEM((8, third), f32),
             pltpu.VMEM((devices, 8, 128), f32),
-            pltpu.SemaphoreType.DMA((8, AXES, CHUNKS)),
-            pltpu.SemaphoreType.DMA((8, AXES, CHUNKS)),
+            pltpu.SemaphoreType.DMA((UNITS, AXES, CHUNKS)),
+            pltpu.SemaphoreType.DMA((UNITS, AXES, CHUNKS)),
             pltpu.SemaphoreType.DMA((AXES, SLOTS)),
-            pltpu.SemaphoreType.DMA((7, AXES, CHUNKS)),
+            pltpu.SemaphoreType.DMA((UNITS - 1, AXES, CHUNKS)),
             pltpu.SemaphoreType.DMA((2, AXES)),
             pltpu.SemaphoreType.DMA((2, AXES)),
+            pltpu.SemaphoreType.DMA((AXES, 2)),
+            pltpu.SemaphoreType.DMA((AXES, 2)),
             pltpu.SemaphoreType.DMA((devices,)),
             pltpu.SemaphoreType.DMA((devices,)),
             pltpu.SemaphoreType.DMA((AXES, CHUNKS)),
@@ -288,11 +326,11 @@
     pieces = rows // PIECE_ROWS
     inputs = (grad, master, first, second)
 
-    def piece_at(owner, i, cols):
-        return working.at[pl.ds(pl.multiple_of(owner * rows + i * PIECE_ROWS, PIECE_ROWS), PIECE_ROWS), cols]
-
-    def send(owner, i, cols, ssem, rsem, target):
-        ref = piece_at(owner, i, cols)
+    def piece_at(owner, i, cols, piece_rows):
+        return working.at[pl.ds(pl.multiple_of(owner * rows + i * piece_rows, piece_rows), piece_rows), cols]
+
+    def send(owner, i, cols, ssem, rsem, target, piece_rows=PIECE_ROWS):
+        ref = piece_at(owner, i, cols, piece_rows)
         return pltpu.make_async_remote_copy(src_ref=ref, dst_ref=ref, send_sem=ssem, recv_sem=rsem,
                                             device_id=(target,), device_id_type=MESH)
 
@@ -325,11 +363,11 @@
 
     def fwd_send(i, kind, k):
         source, axis = hops[kind]
-        return send(chip_flip(*[k + a for a in source]), i, cols_of(k), fwd_ssem.at[kind, k, i], fwd_rsem.at[kind, k, i], chip_flip(k + axis))
+        return send(chip_flip(*[k + a for a in source]), i, cols_of(k), fwd_ssem.at[kind, k, i], fwd_rsem.at[kind, k, i], chip_flip(k + axis), FORWARD_ROWS[kind])
 
     def fwd_recv(i, kind, k):
         source, axis = hops[kind]
-        return send(chip_flip(*[k + a for a in source], k + axis), i, cols_of(k), fwd_ssem.at[kind, k, i], fwd_rsem.at[kind, k, i], chip_flip(k + axis))
+        return send(chip_flip(*[k + a for a in source], k + axis), i, cols_of(k), fwd_ssem.at[kind, k, i], fwd_rsem.at[kind, k, i], chip_flip(k + axis), FORWARD_ROWS[kind])
 
     def pair_own(i, parity=0):
         owner = me if parity == 0 else partner
@@ -345,7 +383,7 @@
         owner = chip_flip(*[k + a for a in source], k + axis)
         owner = owner if parity == 0 else bit_flip(owner, 1)
         slot = 4 + kind * AXES + k
-        return send(owner, i, cols_of(k), pair_ssem.at[slot, i], pair_rsem.at[slot, i], partner)
+        return send(owner, i, cols_of(k), pair_ssem.at[slot, i], pair_rsem.at[slot, i], partner, FORWARD_ROWS[kind])
 
     clip = scale[0, 0]
     learn_rate = rate[0]
@@ -361,8 +399,6 @@
     for t in range(LOADS):
         for n in range(4):
             load(t, n).start()
-    pl.semaphore_wait(barrier, len(peers))
-
     def update_rows(t, carry):
         for n in range(4):
             load(t, n).wait()
@@ -412,24 +448,32 @@
     def own_piece(i, carry):
         per = PIECE_ROWS // LOAD_ROWS
         lax.fori_loop(i * per, (i + 1) * per, update_rows, 0)
+
+        @pl.when(i == 0)
+        def _():
+            pl.semaphore_wait(barrier, len(peers))
         for axis in range(AXES):
             own_send(i, axis).start()
         pair_own(i).start()
         return carry
 
     def neighbour_piece(i, carry):
-        for axis in range(AXES):
-            own_recv(i, axis).wait_recv()
-            pair_axis(i, axis).start()
+        per = FORWARD_ROWS[0] // PIECE_ROWS
+        for part in range(per):
+            for axis in range(AXES):
+                own_recv(i * per + part, axis).wait_recv()
+                pair_axis(i * per + part, axis).start()
         for kind in range(3):
             for k in range(AXES):
                 fwd_send(i, kind, k).start()
         return carry
 
     def far_piece(i, carry):
+        per = FORWARD_ROWS[0] // FORWARD_ROWS[3]
         for k in range(AXES):
             fwd_recv(i, 0, k).wait_recv()
-            fwd_send(i, 3, k).start()
+            for part in range(per):
+                fwd_send(i * per + part, 3, k).start()
             pair_fwd(i, 0, k).start()
         for kind in (1, 2):
             for k in range(AXES):
@@ -443,27 +487,33 @@
             pair_fwd(i, 3, k).start()
         return carry
 
-    def drain(i, carry):
+    def drain_own(i, carry):
         for axis in range(AXES):
             own_send(i, axis).wait_send()
             pair_axis(i, axis).wait_send()
             pair_axis(i, axis, 1).wait_recv()
         pair_own(i).wait_send()
         pair_own(i, 1).wait_recv()
-        for kind in range(4):
+        return carry
+
+    def drain_fwd(i, carry, kinds):
+        for kind in kinds:
             for k in range(AXES):
                 fwd_send(i, kind, k).wait_send()
                 pair_fwd(i, kind, k).wait_send()
                 pair_fwd(i, kind, k, 1).wait_recv()
         return carry
 
+    near_pieces, far_pieces = rows // FORWARD_ROWS[0], rows // FORWARD_ROWS[3]
     lax.fori_loop(0, pieces, own_piece, 0)
-    lax.fori_loop(0, pieces, neighbour_piece, 0)
+    lax.fori_loop(0, near_pieces, neighbour_piece, 0)
     for t in (steps - 2, steps - 1):
         store(t).wait()
-    lax.fori_loop(0, pieces, far_piece, 0)
-    lax.fori_loop(0, pieces, last_piece, 0)
-    lax.fori_loop(0, pieces, drain, 0)
+    lax.fori_loop(0, pieces, drain_own, 0)
+    lax.fori_loop(0, near_pieces, far_piece, 0)
+    lax.fori_loop(0, near_pieces, functools.partial(drain_fwd, kinds=(0, 1, 2)), 0)
+    lax.fori_loop(0, far_pieces, last_piece, 0)
+    lax.fori_loop(0, far_pieces, functools.partial(drain_fwd, kinds=(3,)), 0)
 
 
 def write_kernel(working, new_master, new_first, new_second, working_out, master_out, first_out, second_out,
@@ -522,10 +572,10 @@
             dma((2,)),
             dma((AXES, pieces)),
             dma((AXES, pieces)),
-            dma((4, AXES, pieces)),
-            dma((4, AXES, pieces)),
-            dma((16, pieces)),
-            dma((16, pieces)),
+            dma((4, AXES, rows // min(FORWARD_ROWS))),
+            dma((4, AXES, rows // min(FORWARD_ROWS))),
+            dma((16, rows // min(min(FORWARD_ROWS), PIECE_ROWS))),
+            dma((16, rows // min(min(FORWARD_ROWS), PIECE_ROWS))),
         ],
         compiler_params=pltpu.CompilerParams(has_side_effects=True, vmem_limit_bytes=3 * 1024 * 1024, collective_id=1),
         name='gather',

time: 528 us -> 524 us (level)
  no operation moved by 1% of the time
where the time goes in v4:
time: 524 us; the launch traced here: 522 us
  Pallas kernels  521 us (99%)
    pallas_call x1, Pallas kernels, reduce_scatter(): pl.pallas_call(reduce_kernel, out_shape=(jax.ShapeDtypeStruct((rows, widt...  329 us
    pallas_call x1, Pallas kernels, update_gather(): pl.pallas_call(update_gather_kernel, out_shape=(pltpu.VMEM((devices * row...  168 us
    pallas_call x1, Pallas kernels, update_gather(): pl.pallas_call(write_kernel, out_shape=(working_shape, shard, shard, shar...  23.5 us

profile of v4, /device:TPU:0, one launch (start us, length us, event | category | flops | bytes accessed | tf_op | source)
XLA Modules:
  0.0 522.1 jit_solution(13461006015164350294)
XLA Ops:
  1.3 328.9 %reduce.1 = (f32[2048,768]{1,0:T(8,128)}, f32[8,128]{1,0:T(8,128)}, bf16[7,3,2048,256]{3,2,1,0:T(8,128)(2,1)}) custom-call(bf16[1,32768,768]{2,1,0:T(8,128)(2,1)} %grads.1), custom_call_target="tpu_custom_call" | custom-call | tf_op jit(solution)/shard_map/reduce/pallas_call | solution.py:286
  330.2 168.4 %gather.1 = (bf16[32768,768]{1,0:T(8,128)(2,1)S(1)}, f32[2048,768]{1,0:T(8,128)S(1)}, f32[2048,768]{1,0:T(8,128)S(1)}, f32[2048,768]{1,0:T(8,128)}) custom-call(f32[2048,768]{1,0:T(8,128)} %get-tuple-element.14.grad, f32[2048,768]{1,0:T(8,128)} %master.1, f32[2048,768]{1,0:T(8,128)} %first.1, f32[2048,768]{1,0:T(8,128)} %second.1, ...), custom_call_target="tpu_custom_call" | custom-call | tf_op jit(solution)/shard_map/gather/pallas_call | solution.py:563
  498.6 23.5 %write.1 = (bf16[32768,768]{1,0:T(8,128)(2,1)}, f32[2048,768]{1,0:T(8,128)}, f32[2048,768]{1,0:T(8,128)}, f32[2048,768]{1,0:T(8,128)}) custom-call(bf16[32768,768]{1,0:T(8,128)(2,1)S(1)} %get-tuple-element.16.working, f32[2048,768]{1,0:T(8,128)S(1)} %get-tuple-element.17.new_master, f32[2048,768]{1,0:T(8,128)S(1)} %get-tuple-element.18.new_first, ...), custom_call_target="tpu_custom_call" | custom-call | tf_op jit(solution)/shard_map/write/pallas_call | solution.py:584

commit v5 on v4

--- a/solution.py
+++ b/solution.py
@@ -1,5 +1,3 @@
-import functools
-
 import jax
 import jax.numpy as jnp
 from jax import lax
@@ -17,6 +15,7 @@
 CHUNKS = 4
 SLOTS = 3
 AHEAD = 4
+PAIR_RING = 8
 PIECE_ROWS = 256
 FORWARD_ROWS = (512, 512, 512, 512)
 LOAD_ROWS = 64
@@ -56,7 +55,7 @@
 
 
 def reduce_kernel(grads, g_out, c_out, pairs, landed, raw, stage, own_buf, pair_buf, part_buf, norm_buf,
-                  pair_ssem, pair_rsem, send_sem, recv_sem, own_sem, pairl_sem, raw_ssem, raw_rsem, norm_ssem, norm_rsem, g_sem):
+                  pair_ssem, pair_rsem, send_sem, recv_sem, own_sem, pairl_sem, raw_ssem, raw_rsem, norm_sem, g_sem):
     me = lax.axis_index('dp')
     chip, core = me // 2, me % 2
     partner = bit_flip(me, 1)
@@ -100,8 +99,8 @@
         return pltpu.make_async_remote_copy(
             src_ref=grads.at[0, pl.ds(row, part_rows), pl.ds(k * third, third)],
             dst_ref=pairs.at[j, k, pl.ds(pl.multiple_of(i * part_rows, part_rows), part_rows)],
-            send_sem=pair_ssem.at[j, k, i],
-            recv_sem=pair_rsem.at[j, k, i],
+            send_sem=pair_ssem.at[k],
+            recv_sem=pair_rsem.at[s % PAIR_RING, k],
             device_id=(partner,),
             device_id_type=MESH)
 
@@ -216,13 +215,13 @@
             else:
                 pltpu.make_async_copy(
                     landed.at[0, k, pl.ds(base, part_rows)],
-                    g_out.at[pl.ds(base, part_rows), pl.ds(k * third, third)], g_sem.at[k, i]).start()
+                    g_out.at[pl.ds(base, part_rows), pl.ds(k * third, third)], g_sem.at[k]).start()
         load_next()
 
-    def drain_pair(s, carry):
-        for k in range(AXES):
-            pair_copy(s, k).wait_send()
-        return carry
+    def pairs_sent(k):
+        return pltpu.make_async_remote_copy(
+            src_ref=pairs.at[:, k], dst_ref=pairs.at[:, k], send_sem=pair_ssem.at[k], recv_sem=pair_rsem.at[0, k],
+            device_id=(partner,), device_id_type=MESH)
 
     part_buf[...] = jnp.zeros_like(part_buf)
     for phase, lo, hi in ((1, 0, 3), (2, 3, 5), (3, 5, 6), (4, 6, 7)):
@@ -230,7 +229,8 @@
             step(s, phase)
             return carry
         if phase == 4:
-            lax.fori_loop(0, total_steps, drain_pair, 0)
+            for k in range(AXES):
+                pairs_sent(k).wait_send()
             for k in range(AXES):
                 for parity in range(2):
                     raw_recv(k, parity).wait_recv()
@@ -244,35 +244,24 @@
         return pltpu.make_async_remote_copy(
             src_ref=part_buf.at[:, pl.ds(0, 128)],
             dst_ref=norm_buf.at[me],
-            send_sem=norm_ssem.at[d],
-            recv_sem=norm_rsem.at[me],
+            send_sem=norm_sem.at[0],
+            recv_sem=norm_sem.at[1],
             device_id=((me + d) % devices,),
             device_id_type=MESH)
 
-    def norm_recv(d):
-        sender = (me + devices - d) % devices
-        return pltpu.make_async_remote_copy(
-            src_ref=part_buf.at[:, pl.ds(0, 128)],
-            dst_ref=norm_buf.at[sender],
-            send_sem=norm_ssem.at[d],
-            recv_sem=norm_rsem.at[sender],
-            device_id=(partner,),
-            device_id_type=MESH)
+    norm_all = pltpu.make_async_remote_copy(
+        src_ref=norm_buf.at[pl.ds(1, devices - 1)], dst_ref=norm_buf.at[pl.ds(1, devices - 1)],
+        send_sem=norm_sem.at[0], recv_sem=norm_sem.at[1], device_id=(partner,), device_id_type=MESH)
 
     for d in range(1, devices):
         norm_copy(d).start()
     for last in range(SLOTS):
         for k in range(AXES):
             piece_copy(0, 0, k, last, 0).wait_send()
-    for i in range(CHUNKS):
-        for k in range(AXES):
-            pltpu.make_async_copy(
-                landed.at[0, k, pl.ds(i * part_rows, part_rows)],
-                g_out.at[pl.ds(i * part_rows, part_rows), pl.ds(k * third, third)], g_sem.at[k, i]).wait()
-    for d in range(1, devices):
-        norm_copy(d).wait_send()
-    for d in range(1, devices):
-        norm_recv(d).wait_recv()
+    for k in range(AXES):
+        pltpu.make_async_copy(landed.at[0, k], g_out.at[:, pl.ds(k * third, third)], g_sem.at[k]).wait()
+    norm_all.wait_send()
+    norm_all.wait_recv()
     square_sum = jnp.sum(jnp.sum(norm_buf[...], axis=0), keepdims=True)
     c_out[...] = jnp.broadcast_to(jnp.minimum(1.0, 1.0 / (jnp.sqrt(square_sum) + 1e-6)), c_out.shape)
 
@@ -298,17 +287,16 @@
             pltpu.VMEM((2, AXES, part_rows, third), bf16),
             pltpu.VMEM((8, third), f32),
             pltpu.VMEM((devices, 8, 128), f32),
-            pltpu.SemaphoreType.DMA((UNITS, AXES, CHUNKS)),
-            pltpu.SemaphoreType.DMA((UNITS, AXES, CHUNKS)),
+            pltpu.SemaphoreType.DMA((AXES,)),
+            pltpu.SemaphoreType.DMA((PAIR_RING, AXES)),
             pltpu.SemaphoreType.DMA((AXES, SLOTS)),
             pltpu.SemaphoreType.DMA((UNITS - 1, AXES, CHUNKS)),
             pltpu.SemaphoreType.DMA((2, AXES)),
             pltpu.SemaphoreType.DMA((2, AXES)),
             pltpu.SemaphoreType.DMA((AXES, 2)),
             pltpu.SemaphoreType.DMA((AXES, 2)),
-            pltpu.SemaphoreType.DMA((devices,)),
-            pltpu.SemaphoreType.DMA((devices,)),
-            pltpu.SemaphoreType.DMA((AXES, CHUNKS)),
+            pltpu.SemaphoreType.DMA((2,)),
+            pltpu.SemaphoreType.DMA((AXES,)),
         ],
         compiler_params=pltpu.CompilerParams(has_side_effects=True, vmem_limit_bytes=60 * 1024 * 1024, collective_id=0),
         name='reduce',
@@ -354,36 +342,34 @@
         return pltpu.make_async_copy(out_buf.at[t % 2], new_second.at[here], out_sem.at[t % 2])
 
     def own_send(i, axis):
-        return send(me, i, every, own_ssem.at[axis, i], own_rsem.at[axis, i], chip_flip(axis))
+        return send(me, i, every, own_ssem.at[axis], own_rsem.at[axis, i], chip_flip(axis))
 
     def own_recv(i, axis):
-        return send(chip_flip(axis), i, every, own_ssem.at[axis, i], own_rsem.at[axis, i], chip_flip(axis))
+        return send(chip_flip(axis), i, every, own_ssem.at[axis], own_rsem.at[axis, i], chip_flip(axis))
 
     hops = (((0,), 1), ((0,), 2), ((1,), 2), ((0, 1), 2))
 
     def fwd_send(i, kind, k):
         source, axis = hops[kind]
-        return send(chip_flip(*[k + a for a in source]), i, cols_of(k), fwd_ssem.at[kind, k, i], fwd_rsem.at[kind, k, i], chip_flip(k + axis), FORWARD_ROWS[kind])
+        return send(chip_flip(*[k + a for a in source]), i, cols_of(k), fwd_ssem.at[kind], fwd_rsem.at[kind, k, i], chip_flip(k + axis), FORWARD_ROWS[kind])
 
     def fwd_recv(i, kind, k):
         source, axis = hops[kind]
-        return send(chip_flip(*[k + a for a in source], k + axis), i, cols_of(k), fwd_ssem.at[kind, k, i], fwd_rsem.at[kind, k, i], chip_flip(k + axis), FORWARD_ROWS[kind])
-
-    def pair_own(i, parity=0):
-        owner = me if parity == 0 else partner
-        return send(owner, i, every, pair_ssem.at[0, i], pair_rsem.at[0, i], partner)
-
-    def pair_axis(i, axis, parity=0):
-        owner = chip_flip(axis)
-        owner = owner if parity == 0 else bit_flip(owner, 1)
-        return send(owner, i, every, pair_ssem.at[1 + axis, i], pair_rsem.at[1 + axis, i], partner)
-
-    def pair_fwd(i, kind, k, parity=0):
+        return send(chip_flip(*[k + a for a in source], k + axis), i, cols_of(k), fwd_ssem.at[kind], fwd_rsem.at[kind, k, i], chip_flip(k + axis), FORWARD_ROWS[kind])
+
+    def pair_own(i):
+        return send(me, i, every, pair_ssem.at[0], pair_rsem.at[0], partner)
+
+    def pair_axis(i, axis):
+        return send(chip_flip(axis), i, every, pair_ssem.at[1 + axis], pair_rsem.at[1 + axis], partner)
+
+    def pair_fwd(i, kind, k):
         source, axis = hops[kind]
         owner = chip_flip(*[k + a for a in source], k + axis)
-        owner = owner if parity == 0 else bit_flip(owner, 1)
-        slot = 4 + kind * AXES + k
-        return send(owner, i, cols_of(k), pair_ssem.at[slot, i], pair_rsem.at[slot, i], partner, FORWARD_ROWS[kind])
+        return send(owner, i, cols_of(k), pair_ssem.at[4 + kind], pair_rsem.at[4 + kind], partner, FORWARD_ROWS[kind])
+
+    def whole(ssem, rsem):
+        return send(me, 0, every, ssem, rsem, partner, rows)
 
     clip = scale[0, 0]
     learn_rate = rate[0]
@@ -487,33 +473,29 @@
             pair_fwd(i, 3, k).start()
         return carry
 
-    def drain_own(i, carry):
+    def drain_own():
         for axis in range(AXES):
-            own_send(i, axis).wait_send()
-            pair_axis(i, axis).wait_send()
-            pair_axis(i, axis, 1).wait_recv()
-        pair_own(i).wait_send()
-        pair_own(i, 1).wait_recv()
-        return carry
-
-    def drain_fwd(i, carry, kinds):
+            whole(own_ssem.at[axis], own_rsem.at[axis, 0]).wait_send()
+        for slot in range(4):
+            whole(pair_ssem.at[slot], pair_rsem.at[slot]).wait_send()
+            whole(pair_ssem.at[slot], pair_rsem.at[slot]).wait_recv()
+
+    def drain_fwd(kinds):
         for kind in kinds:
-            for k in range(AXES):
-                fwd_send(i, kind, k).wait_send()
-                pair_fwd(i, kind, k).wait_send()
-                pair_fwd(i, kind, k, 1).wait_recv()
-        return carry
+            whole(fwd_ssem.at[kind], fwd_rsem.at[kind, 0, 0]).wait_send()
+            whole(pair_ssem.at[4 + kind], pair_rsem.at[4 + kind]).wait_send()
+            whole(pair_ssem.at[4 + kind], pair_rsem.at[4 + kind]).wait_recv()
 
     near_pieces, far_pieces = rows // FORWARD_ROWS[0], rows // FORWARD_ROWS[3]
     lax.fori_loop(0, pieces, own_piece, 0)
     lax.fori_loop(0, near_pieces, neighbour_piece, 0)
     for t in (steps - 2, steps - 1):
         store(t).wait()
-    lax.fori_loop(0, pieces, drain_own, 0)
+    drain_own()
     lax.fori_loop(0, near_pieces, far_piece, 0)
-    lax.fori_loop(0, near_pieces, functools.partial(drain_fwd, kinds=(0, 1, 2)), 0)
+    drain_fwd((0, 1, 2))
     lax.fori_loop(0, far_pieces, last_piece, 0)
-    lax.fori_loop(0, far_pieces, functools.partial(drain_fwd, kinds=(3,)), 0)
+    drain_fwd((3,))
 
 
 def write_kernel(working, new_master, new_first, new_second, working_out, master_out, first_out, second_out,
@@ -570,12 +552,12 @@
             pltpu.VMEM((2, LOAD_ROWS, width), f32),
             dma((LOADS, 4)),
             dma((2,)),
+            dma((AXES,)),
             dma((AXES, pieces)),
-            dma((AXES, pieces)),
+            dma((4,)),
             dma((4, AXES, rows // min(FORWARD_ROWS))),
-            dma((4, AXES, rows // min(FORWARD_ROWS))),
-            dma((16, rows // min(min(FORWARD_ROWS), PIECE_ROWS))),
-            dma((16, rows // min(min(FORWARD_ROWS), PIECE_ROWS))),
+            dma((8,)),
+            dma((8,)),
         ],
         compiler_params=pltpu.CompilerParams(has_side_effects=True, vmem_limit_bytes=3 * 1024 * 1024, collective_id=1),
         name='gather',

time: 524 us -> 519 us (level)
  no operation moved by 1% of the time
where the time goes in v5:
time: 519 us; the launch traced here: 518 us
  Pallas kernels  516 us (99%)
    pallas_call x1, Pallas kernels, reduce_scatter(): pl.pallas_call(reduce_kernel, out_shape=(jax.ShapeDtypeStruct((rows, widt...  327 us
    pallas_call x1, Pallas kernels, update_gather(): pl.pallas_call(update_gather_kernel, out_shape=(pltpu.VMEM((devices * row...  166 us
    pallas_call x1, Pallas kernels, update_gather(): pl.pallas_call(write_kernel, out_shape=(working_shape, shard, shard, shar...  23.5 us

profile of v5, /device:TPU:0, one launch (start us, length us, event | category | flops | bytes accessed | tf_op | source)
XLA Modules:
  0.0 517.8 jit_solution(8745470574266347192)
XLA Ops:
  1.3 327.3 %reduce.1 = (f32[2048,768]{1,0:T(8,128)}, f32[8,128]{1,0:T(8,128)}, bf16[7,3,2048,256]{3,2,1,0:T(8,128)(2,1)}) custom-call(bf16[1,32768,768]{2,1,0:T(8,128)(2,1)} %grads.1), custom_call_target="tpu_custom_call" | custom-call | tf_op jit(solution)/shard_map/reduce/pallas_call | solution.py:275
  328.6 165.7 %gather.1 = (bf16[32768,768]{1,0:T(8,128)(2,1)S(1)}, f32[2048,768]{1,0:T(8,128)S(1)}, f32[2048,768]{1,0:T(8,128)S(1)}, f32[2048,768]{1,0:T(8,128)}) custom-call(f32[2048,768]{1,0:T(8,128)} %get-tuple-element.14.grad, f32[2048,768]{1,0:T(8,128)} %master.1, f32[2048,768]{1,0:T(8,128)} %first.1, f32[2048,768]{1,0:T(8,128)} %second.1, ...), custom_call_target="tpu_custom_call" | custom-call | tf_op jit(solution)/shard_map/gather/pallas_call | solution.py:545
  494.2 23.5 %write.1 = (bf16[32768,768]{1,0:T(8,128)(2,1)}, f32[2048,768]{1,0:T(8,128)}, f32[2048,768]{1,0:T(8,128)}, f32[2048,768]{1,0:T(8,128)}) custom-call(bf16[32768,768]{1,0:T(8,128)(2,1)S(1)} %get-tuple-element.16.working, f32[2048,768]{1,0:T(8,128)S(1)} %get-tuple-element.17.new_master, f32[2048,768]{1,0:T(8,128)S(1)} %get-tuple-element.18.new_first, ...), custom_call_target="tpu_custom_call" | custom-call | tf_op jit(solution)/shard_map/write/pallas_call | solution.py:566

commit v6 on v5

--- a/solution.py
+++ b/solution.py
@@ -13,13 +13,14 @@
 AXES = 3
 UNITS = 7
 CHUNKS = 4
+SUBS = 2
 SLOTS = 3
 AHEAD = 4
 PAIR_RING = 8
 PIECE_ROWS = 256
-FORWARD_ROWS = (512, 512, 512, 512)
-LOAD_ROWS = 64
-LOADS = 3
+FORWARD_ROWS = (512, 512, 512, 256)
+LOAD_ROWS = 32
+LOADS = 6
 MESH = pl.DeviceIdType.MESH
 
 
@@ -55,7 +56,7 @@
 
 
 def reduce_kernel(grads, g_out, c_out, pairs, landed, raw, stage, own_buf, pair_buf, part_buf, norm_buf,
-                  pair_ssem, pair_rsem, send_sem, recv_sem, own_sem, pairl_sem, raw_ssem, raw_rsem, norm_sem, g_sem):
+                  pair_ssem, pair_rsem, send_sem, recv_sem, last_sem, own_sem, pairl_sem, raw_ssem, raw_rsem, norm_sem, g_sem):
     me = lax.axis_index('dp')
     chip, core = me // 2, me % 2
     partner = bit_flip(me, 1)
@@ -115,14 +116,30 @@
         return pltpu.make_async_copy(
             pairs.at[j, k, pl.ds(pl.multiple_of(i * part_rows, part_rows), part_rows)], pair_buf.at[s % 2, k], pairl_sem.at[s % 2, k])
 
+    sub_rows = part_rows // SUBS
+
     def piece_copy(j, i, k, slot, axis):
         return pltpu.make_async_remote_copy(
             src_ref=stage.at[k, slot],
             dst_ref=landed.at[j, k, pl.ds(pl.multiple_of(i * part_rows, part_rows), part_rows)],
             send_sem=send_sem.at[k, slot],
-            recv_sem=recv_sem.at[j, k, i],
+            recv_sem=recv_sem.at[j, k],
             device_id=(bit_flip(me, 2 << axis),),
             device_id_type=MESH)
+
+    def last_copy(i, sub, k, slot, axis):
+        return pltpu.make_async_remote_copy(
+            src_ref=stage.at[k, slot, pl.ds(sub * sub_rows, sub_rows)],
+            dst_ref=landed.at[UNITS - 2, k, pl.ds(pl.multiple_of(i * part_rows + sub * sub_rows, sub_rows), sub_rows)],
+            send_sem=send_sem.at[k, slot],
+            recv_sem=last_sem.at[k, i, sub],
+            device_id=(bit_flip(me, 2 << axis),),
+            device_id_type=MESH)
+
+    def unit_recv(j, k):
+        return pltpu.make_async_remote_copy(
+            src_ref=landed.at[j, k], dst_ref=landed.at[j, k], send_sem=send_sem.at[k, 0], recv_sem=recv_sem.at[j, k],
+            device_id=(partner,), device_id_type=MESH)
 
     total_steps = UNITS * CHUNKS
 
@@ -184,35 +201,42 @@
         for k in range(AXES):
             own_load(s, k).wait()
             pair_load(s, k).wait()
-            for source in sources:
-                piece_copy(source, i, k, 0, 0).wait_recv()
             if phase < 4:
                 @pl.when(s >= SLOTS)
                 def _():
                     piece_copy(0, 0, k, slot, 0).wait_send()
-            group = 64
-
-            def add_rows(r, carry):
-                lo = pl.multiple_of(r * group, group)
-                value = own_buf[s % 2, k, pl.ds(lo, group)].astype(jnp.float32) + pair_buf[s % 2, k, pl.ds(lo, group)].astype(jnp.float32)
-                for source in sources:
-                    value = value + landed[source, k, pl.ds(base + lo, group)]
+        subs = SUBS if phase > 2 else 1
+        count = part_rows // subs
+        group = 64
+        for sub in range(subs):
+            for k in range(AXES):
+                if phase == 4:
+                    last_copy(i, sub, k, 0, 0).wait_recv()
+
+                def add_rows(r, carry):
+                    lo = pl.multiple_of(sub * count + r * group, group)
+                    value = own_buf[s % 2, k, pl.ds(lo, group)].astype(jnp.float32) + pair_buf[s % 2, k, pl.ds(lo, group)].astype(jnp.float32)
+                    for source in sources:
+                        value = value + landed[source, k, pl.ds(base + lo, group)]
+                    if phase < 4:
+                        stage[k, slot, pl.ds(lo, group)] = value
+                        return carry
+                    for parity in range(2):
+                        value = value + raw[k, parity, pl.ds(base + lo, group)].astype(jnp.float32)
+                    value = value * (1.0 / devices)
+                    landed[0, k, pl.ds(base + lo, group)] = value
+                    return carry + jnp.sum((value * value).reshape(group // 8, 8, third), axis=0)
+
                 if phase < 4:
-                    stage[k, slot, pl.ds(lo, group)] = value
-                    return carry
-                for parity in range(2):
-                    value = value + raw[k, parity, pl.ds(base + lo, group)].astype(jnp.float32)
-                value = value * (1.0 / devices)
-                landed[0, k, pl.ds(base + lo, group)] = value
-                return carry + jnp.sum((value * value).reshape(group // 8, 8, third), axis=0)
-
-            if phase < 4:
-                lax.fori_loop(0, part_rows // group, add_rows, 0)
-            else:
-                part_buf[...] += lax.fori_loop(0, part_rows // group, add_rows, jnp.zeros((8, third), jnp.float32))
-            if phase < 4:
-                piece_copy(j, i, k, slot, (k + phase - 1) % AXES).start()
-            else:
+                    lax.fori_loop(0, count // group, add_rows, 0)
+                else:
+                    part_buf[...] += lax.fori_loop(0, count // group, add_rows, jnp.zeros((8, third), jnp.float32))
+                if phase < 3:
+                    piece_copy(j, i, k, slot, (k + phase - 1) % AXES).start()
+                elif phase == 3:
+                    last_copy(i, sub, k, slot, (k + phase - 1) % AXES).start()
+        if phase == 4:
+            for k in range(AXES):
                 pltpu.make_async_copy(
                     landed.at[0, k, pl.ds(base, part_rows)],
                     g_out.at[pl.ds(base, part_rows), pl.ds(k * third, third)], g_sem.at[k]).start()
@@ -228,6 +252,9 @@
         def run(s, carry, phase=phase):
             step(s, phase)
             return carry
+        for source in ([], [0, 1], [2, 3], [4])[phase - 1]:
+            for k in range(AXES):
+                unit_recv(source, k).wait_recv()
         if phase == 4:
             for k in range(AXES):
                 pairs_sent(k).wait_send()
@@ -290,7 +317,8 @@
             pltpu.SemaphoreType.DMA((AXES,)),
             pltpu.SemaphoreType.DMA((PAIR_RING, AXES)),
             pltpu.SemaphoreType.DMA((AXES, SLOTS)),
-            pltpu.SemaphoreType.DMA((UNITS - 1, AXES, CHUNKS)),
+            pltpu.SemaphoreType.DMA((UNITS - 2, AXES)),
+            pltpu.SemaphoreType.DMA((AXES, CHUNKS, SUBS)),
             pltpu.SemaphoreType.DMA((2, AXES)),
             pltpu.SemaphoreType.DMA((2, AXES)),
             pltpu.SemaphoreType.DMA((AXES, 2)),
@@ -316,6 +344,9 @@
 
     def piece_at(owner, i, cols, piece_rows):
         return working.at[pl.ds(pl.multiple_of(owner * rows + i * piece_rows, piece_rows), piece_rows), cols]
+
+    def first_send(t, axis):
+        return send(me, t, every, own_ssem.at[axis], own_rsem.at[axis, 0], chip_flip(axis), LOAD_ROWS)
 
     def send(owner, i, cols, ssem, rsem, target, piece_rows=PIECE_ROWS):
         ref = piece_at(owner, i, cols, piece_rows)
@@ -434,10 +465,6 @@
     def own_piece(i, carry):
         per = PIECE_ROWS // LOAD_ROWS
         lax.fori_loop(i * per, (i + 1) * per, update_rows, 0)
-
-        @pl.when(i == 0)
-        def _():
-            pl.semaphore_wait(barrier, len(peers))
         for axis in range(AXES):
             own_send(i, axis).start()
         pair_own(i).start()
@@ -487,7 +514,14 @@
             whole(pair_ssem.at[4 + kind], pair_rsem.at[4 + kind]).wait_recv()
 
     near_pieces, far_pieces = rows // FORWARD_ROWS[0], rows // FORWARD_ROWS[3]
-    lax.fori_loop(0, pieces, own_piece, 0)
+    for t in range(PIECE_ROWS // LOAD_ROWS):
+        update_rows(t, 0)
+        if t == 0:
+            pl.semaphore_wait(barrier, len(peers))
+        for axis in range(AXES):
+            first_send(t, axis).start()
+    pair_own(0).start()
+    lax.fori_loop(1, pieces, own_piece, 0)
     lax.fori_loop(0, near_pieces, neighbour_piece, 0)
     for t in (steps - 2, steps - 1):
         store(t).wait()

time: 519 us -> 516 us (level)
  no operation moved by 1% of the time
where the time goes in v6:
time: 516 us; the launch traced here: 515 us
  Pallas kernels  514 us (100%)
    pallas_call x1, Pallas kernels, reduce_scatter(): pl.pallas_call(reduce_kernel, out_shape=(jax.ShapeDtypeStruct((rows, widt...  327 us
    pallas_call x1, Pallas kernels, update_gather(): pl.pallas_call(update_gather_kernel, out_shape=(pltpu.VMEM((devices * row...  164 us
    pallas_call x1, Pallas kernels, update_gather(): pl.pallas_call(write_kernel, out_shape=(working_shape, shard, shard, shar...  23.5 us

profile of v6, /device:TPU:0, one launch (start us, length us, event | category | flops | bytes accessed | tf_op | source)
XLA Modules:
  0.0 515.2 jit_solution(9881801152855219527)
XLA Ops:
  1.3 326.6 %reduce.1 = (f32[2048,768]{1,0:T(8,128)}, f32[8,128]{1,0:T(8,128)}, bf16[7,3,2048,256]{3,2,1,0:T(8,128)(2,1)}) custom-call(bf16[1,32768,768]{2,1,0:T(8,128)(2,1)} %grads.1), custom_call_target="tpu_custom_call" | custom-call | tf_op jit(solution)/shard_map/reduce/pallas_call | solution.py:302
  327.8 163.8 %gather.1 = (bf16[32768,768]{1,0:T(8,128)(2,1)S(1)}, f32[2048,768]{1,0:T(8,128)S(1)}, f32[2048,768]{1,0:T(8,128)S(1)}, f32[2048,768]{1,0:T(8,128)}) custom-call(f32[2048,768]{1,0:T(8,128)} %get-tuple-element.14.grad, f32[2048,768]{1,0:T(8,128)} %master.1, f32[2048,768]{1,0:T(8,128)} %first.1, f32[2048,768]{1,0:T(8,128)} %second.1, ...), custom_call_target="tpu_custom_call" | custom-call | tf_op jit(solution)/shard_map/gather/pallas_call | solution.py:579
  491.6 23.5 %write.1 = (bf16[32768,768]{1,0:T(8,128)(2,1)}, f32[2048,768]{1,0:T(8,128)}, f32[2048,768]{1,0:T(8,128)}, f32[2048,768]{1,0:T(8,128)}) custom-call(bf16[32768,768]{1,0:T(8,128)(2,1)S(1)} %get-tuple-element.16.working, f32[2048,768]{1,0:T(8,128)S(1)} %get-tuple-element.17.new_master, f32[2048,768]{1,0:T(8,128)S(1)} %get-tuple-element.18.new_first, ...), custom_call_target="tpu_custom_call" | custom-call | tf_op jit(solution)/shard_map/write/pallas_call | solution.py:600

commit v7 on v6

--- a/solution.py
+++ b/solution.py
@@ -273,14 +273,14 @@
             dst_ref=norm_buf.at[me],
             send_sem=norm_sem.at[0],
             recv_sem=norm_sem.at[1],
-            device_id=((me + d) % devices,),
+            device_id=(bit_flip(me, d),),
             device_id_type=MESH)
 
     norm_all = pltpu.make_async_remote_copy(
         src_ref=norm_buf.at[pl.ds(1, devices - 1)], dst_ref=norm_buf.at[pl.ds(1, devices - 1)],
         send_sem=norm_sem.at[0], recv_sem=norm_sem.at[1], device_id=(partner,), device_id_type=MESH)
 
-    for d in range(1, devices):
+    for d in sorted(range(1, devices), key=lambda d: -bin(d // 2).count('1')):
         norm_copy(d).start()
     for last in range(SLOTS):
         for k in range(AXES):
@@ -333,7 +333,7 @@
 
 
 def update_gather_kernel(grad, master, first, second, scale, rate, working, new_master, new_first, new_second,
-                         in_buf, out_buf, in_sem, out_sem, own_ssem, own_rsem, fwd_ssem, fwd_rsem, pair_ssem, pair_rsem):
+                         in_buf, out_buf, rate_buf, scale_buf, small_sem, in_sem, out_sem, own_ssem, own_rsem, fwd_ssem, fwd_rsem, pair_ssem, pair_rsem):
     me = lax.axis_index('dp')
     partner = bit_flip(me, 1)
     rows, width = grad.shape
@@ -378,15 +378,16 @@
     def own_recv(i, axis):
         return send(chip_flip(axis), i, every, own_ssem.at[axis], own_rsem.at[axis, i], chip_flip(axis))
 
+    fwd_base = [AXES * sum(rows // n for n in FORWARD_ROWS[:kind]) for kind in range(4)]
     hops = (((0,), 1), ((0,), 2), ((1,), 2), ((0, 1), 2))
 
     def fwd_send(i, kind, k):
         source, axis = hops[kind]
-        return send(chip_flip(*[k + a for a in source]), i, cols_of(k), fwd_ssem.at[kind], fwd_rsem.at[kind, k, i], chip_flip(k + axis), FORWARD_ROWS[kind])
+        return send(chip_flip(*[k + a for a in source]), i, cols_of(k), fwd_ssem.at[kind], fwd_rsem.at[fwd_base[kind] + k * (rows // FORWARD_ROWS[kind]) + i], chip_flip(k + axis), FORWARD_ROWS[kind])
 
     def fwd_recv(i, kind, k):
         source, axis = hops[kind]
-        return send(chip_flip(*[k + a for a in source], k + axis), i, cols_of(k), fwd_ssem.at[kind], fwd_rsem.at[kind, k, i], chip_flip(k + axis), FORWARD_ROWS[kind])
+        return send(chip_flip(*[k + a for a in source], k + axis), i, cols_of(k), fwd_ssem.at[kind], fwd_rsem.at[fwd_base[kind] + k * (rows // FORWARD_ROWS[kind]) + i], chip_flip(k + axis), FORWARD_ROWS[kind])
 
     def pair_own(i):
         return send(me, i, every, pair_ssem.at[0], pair_rsem.at[0], partner)
@@ -402,13 +403,14 @@
     def whole(ssem, rsem):
         return send(me, 0, every, ssem, rsem, partner, rows)
 
-    clip = scale[0, 0]
-    learn_rate = rate[0]
     run_starts, lr_values, decay_values = layout_runs(width, total_rows)
     first_norm = 1.0 / (1.0 - 0.9 ** ADAM_STEP)
     second_norm = 1.0 / (1.0 - 0.99 ** ADAM_STEP)
 
     steps = rows // LOAD_ROWS
+    small = (pltpu.make_async_copy(scale, scale_buf, small_sem.at[0]), pltpu.make_async_copy(rate, rate_buf, small_sem.at[1]))
+    for copy in small:
+        copy.start()
     barrier = pltpu.get_barrier_semaphore()
     peers = [partner] + [chip_flip(axis) for axis in range(AXES)]
     for peer in peers:
@@ -439,10 +441,10 @@
                 past = row_ids >= r_start
                 factor = jnp.where(past, r_lr, factor)
                 decay = jnp.where(past, r_decay, decay)
-            step_size = learn_rate * factor
+            step_size = rate_buf[...] * factor
             for tile in range(width // 128):
                 at = pl.ds(tile * 128, 128)
-                clipped = in_buf[slot, 0, here, at] * clip
+                clipped = in_buf[slot, 0, here, at] * scale_buf[pl.ds(0, 1)]
                 weights = in_buf[slot, 1, here, at]
                 moment = 0.9 * in_buf[slot, 2, here, at] + 0.1 * clipped
                 square = 0.99 * in_buf[slot, 3, here, at] + 0.01 * (clipped * clipped)
@@ -509,11 +511,13 @@
 
     def drain_fwd(kinds):
         for kind in kinds:
-            whole(fwd_ssem.at[kind], fwd_rsem.at[kind, 0, 0]).wait_send()
+            whole(fwd_ssem.at[kind], fwd_rsem.at[fwd_base[kind]]).wait_send()
             whole(pair_ssem.at[4 + kind], pair_rsem.at[4 + kind]).wait_send()
             whole(pair_ssem.at[4 + kind], pair_rsem.at[4 + kind]).wait_recv()
 
     near_pieces, far_pieces = rows // FORWARD_ROWS[0], rows // FORWARD_ROWS[3]
+    for copy in small:
+        copy.wait()
     for t in range(PIECE_ROWS // LOAD_ROWS):
         update_rows(t, 0)
         if t == 0:
@@ -579,23 +583,26 @@
     working, new_master, new_first, new_second = pl.pallas_call(
         update_gather_kernel,
         out_shape=(pltpu.VMEM((devices * rows, width), bf16), near, near, shard),
-        in_specs=[any_spec] * 4 + [vmem_spec, pl.BlockSpec(memory_space=pltpu.SMEM)],
+        in_specs=[any_spec] * 6,
         out_specs=(vmem_spec, vmem_spec, vmem_spec, any_spec),
         scratch_shapes=[
             pltpu.VMEM((LOADS, 4, LOAD_ROWS, width), f32),
             pltpu.VMEM((2, LOAD_ROWS, width), f32),
+            pltpu.VMEM((1, 128), f32),
+            pltpu.VMEM((8, 128), f32),
+            dma((2,)),
             dma((LOADS, 4)),
             dma((2,)),
             dma((AXES,)),
             dma((AXES, pieces)),
             dma((4,)),
-            dma((4, AXES, rows // min(FORWARD_ROWS))),
+            dma((AXES * sum(rows // n for n in FORWARD_ROWS),)),
             dma((8,)),
             dma((8,)),
         ],
         compiler_params=pltpu.CompilerParams(has_side_effects=True, vmem_limit_bytes=3 * 1024 * 1024, collective_id=1),
         name='gather',
-    )(grad, master, first, second, scale, rate.reshape(1))
+    )(grad, master, first, second, scale, jnp.broadcast_to(rate, (1, 128)))
     working_shape = pltpu.HBM((devices * rows, width), bf16)
     return pl.pallas_call(
         write_kernel,

time: 516 us -> 516 us (level)
  no operation moved by 1% of the time
where the time goes in v7:
time: 516 us; the launch traced here: 515 us
  Pallas kernels  513 us (99%)
    pallas_call x1, Pallas kernels, reduce_scatter(): pl.pallas_call(reduce_kernel, out_shape=(jax.ShapeDtypeStruct((rows, widt...  326 us
    pallas_call x1, Pallas kernels, update_gather(): pl.pallas_call(update_gather_kernel, out_shape=(pltpu.VMEM((devices * row...  163 us
    pallas_call x1, Pallas kernels, update_gather(): pl.pallas_call(write_kernel, out_shape=(working_shape, shard, shard, shar...  23.5 us

profile of v7, /device:TPU:0, one launch (start us, length us, event | category | flops | bytes accessed | tf_op | source)
XLA Modules:
  0.0 514.6 jit_solution(7171594523176465686)
XLA Ops:
  1.3 0.5 broadcast_in_dim.3.rate
  1.8 326.5 %reduce.1 = (f32[2048,768]{1,0:T(8,128)}, f32[8,128]{1,0:T(8,128)}, bf16[7,3,2048,256]{3,2,1,0:T(8,128)(2,1)}) custom-call(bf16[1,32768,768]{2,1,0:T(8,128)(2,1)} %grads.1), custom_call_target="tpu_custom_call" | custom-call | tf_op jit(solution)/shard_map/reduce/pallas_call | solution.py:302
  328.3 162.8 %gather.1 = (bf16[32768,768]{1,0:T(8,128)(2,1)S(1)}, f32[2048,768]{1,0:T(8,128)S(1)}, f32[2048,768]{1,0:T(8,128)S(1)}, f32[2048,768]{1,0:T(8,128)}) custom-call(f32[2048,768]{1,0:T(8,128)} %get-tuple-element.14.grad, f32[2048,768]{1,0:T(8,128)} %master.1, f32[2048,768]{1,0:T(8,128)} %first.1, f32[2048,768]{1,0:T(8,128)} %second.1, ...), custom_call_target="tpu_custom_call" | custom-call | tf_op jit(solution)/shard_map/gather/pallas_call | solution.py:583
  491.1 23.5 %write.1 = (bf16[32768,768]{1,0:T(8,128)(2,1)}, f32[2048,768]{1,0:T(8,128)}, f32[2048,768]{1,0:T(8,128)}, f32[2048,768]{1,0:T(8,128)}) custom-call(bf16[32768,768]{1,0:T(8,128)(2,1)S(1)} %get-tuple-element.16.working, f32[2048,768]{1,0:T(8,128)S(1)} %get-tuple-element.17.new_master, f32[2048,768]{1,0:T(8,128)S(1)} %get-tuple-element.18.new_first, ...), custom_call_target="tpu_custom_call" | custom-call | tf_op jit(solution)/shard_map/write/pallas_call | solution.py:607

commit v8 on v7

--- a/solution.py
+++ b/solution.py
@@ -17,7 +17,7 @@
 SLOTS = 3
 AHEAD = 4
 PAIR_RING = 8
-PIECE_ROWS = 256
+PIECE_ROWS = 512
 FORWARD_ROWS = (512, 512, 512, 256)
 LOAD_ROWS = 32
 LOADS = 6

time: 516 us -> 516 us (level)
  no operation moved by 1% of the time
where the time goes in v8:
time: 516 us; the launch traced here: 515 us
  Pallas kernels  513 us (99%)
    pallas_call x1, Pallas kernels, reduce_scatter(): pl.pallas_call(reduce_kernel, out_shape=(jax.ShapeDtypeStruct((rows, widt...  326 us
    pallas_call x1, Pallas kernels, update_gather(): pl.pallas_call(update_gather_kernel, out_shape=(pltpu.VMEM((devices * row...  163 us
    pallas_call x1, Pallas kernels, update_gather(): pl.pallas_call(write_kernel, out_shape=(working_shape, shard, shard, shar...  23.5 us

profile of v8, /device:TPU:0, one launch (start us, length us, event | category | flops | bytes accessed | tf_op | source)
XLA Modules:
  0.0 514.5 jit_solution(9345727077814137314)
XLA Ops:
  1.3 0.5 broadcast_in_dim.3.rate
  1.8 326.5 %reduce.1 = (f32[2048,768]{1,0:T(8,128)}, f32[8,128]{1,0:T(8,128)}, bf16[7,3,2048,256]{3,2,1,0:T(8,128)(2,1)}) custom-call(bf16[1,32768,768]{2,1,0:T(8,128)(2,1)} %grads.1), custom_call_target="tpu_custom_call" | custom-call | tf_op jit(solution)/shard_map/reduce/pallas_call | solution.py:302
  328.3 162.7 %gather.1 = (bf16[32768,768]{1,0:T(8,128)(2,1)S(1)}, f32[2048,768]{1,0:T(8,128)S(1)}, f32[2048,768]{1,0:T(8,128)S(1)}, f32[2048,768]{1,0:T(8,128)}) custom-call(f32[2048,768]{1,0:T(8,128)} %get-tuple-element.14.grad, f32[2048,768]{1,0:T(8,128)} %master.1, f32[2048,768]{1,0:T(8,128)} %first.1, f32[2048,768]{1,0:T(8,128)} %second.1, ...), custom_call_target="tpu_custom_call" | custom-call | tf_op jit(solution)/shard_map/gather/pallas_call | solution.py:583
  491.0 23.5 %write.1 = (bf16[32768,768]{1,0:T(8,128)(2,1)}, f32[2048,768]{1,0:T(8,128)}, f32[2048,768]{1,0:T(8,128)}, f32[2048,768]{1,0:T(8,128)}) custom-call(bf16[32768,768]{1,0:T(8,128)(2,1)S(1)} %get-tuple-element.16.working, f32[2048,768]{1,0:T(8,128)S(1)} %get-tuple-element.17.new_master, f32[2048,768]{1,0:T(8,128)S(1)} %get-tuple-element.18.new_first, ...), custom_call_target="tpu_custom_call" | custom-call | tf_op jit(solution)/shard_map/write/pallas_call | solution.py:607
